TPU v7x, 32 devices: a whole 2x2x4 slice. The times are simulated.
32 devices in a mesh: dp: 2 (over x), sp: 16 (over z, y, core).
Axes of the slice: x: 2, y: 2, z: 4, core: 2. Of those that a mesh axis runs over, the one named last changes fastest.
Arguments:
- x_in: bfloat16 [24576, 1024], P(('dp', 'sp')), parts along dimension 0
- w_q: bfloat16 [1024, 1024], replicated
- w_k: bfloat16 [1024, 1024], replicated
- w_v: bfloat16 [1024, 1024], replicated
- w_o: bfloat16 [1024, 1024], replicated
- dy_in: bfloat16 [24576, 1024], P(('dp', 'sp')), parts along dimension 0
Outputs:
- output 1: bfloat16 [24576, 1024], P(('dp', 'sp')), parts along dimension 0
- output 2: bfloat16 [24576, 1024], P(('dp', 'sp')), parts along dimension 0
- output 3: float32 [2048, 1024], P('dp'), parts along dimension 0
- output 4: float32 [2048, 1024], P('dp'), parts along dimension 0
- output 5: float32 [2048, 1024], P('dp'), parts along dimension 0
- output 6: float32 [2048, 1024], P('dp'), parts along dimension 0
There are 2 independent parts. A program takes and returns all parts, laid end to end along the dimension named above; an argument that names none is the same for every part.
All inputs are finite; a program needn't handle non-finite values.
Results may differ from a plain program's by a relative error of at most 0.0125486.
Values are sent between devices in bfloat16 or wider.
A program may use at most 1 GiB of HBM per device.

v0:
```python
import jax
import jax.numpy as jnp
from jax import lax
from jax.sharding import PartitionSpec as P

HEAD_DIM = 64
DILATIONS = (1, 2, 4, 8)


def pick_rows(values, dilation):
    n_rows, model_dim = values.shape
    groups = model_dim // (dilation * HEAD_DIM)
    split_view = values.reshape(n_rows // dilation, dilation, groups, dilation, HEAD_DIM)
    return jnp.stack([split_view[:, residue, :, residue, :] for residue in range(dilation)], axis=2)


def pick_stats(values, dilation):
    n_rows, n_heads = values.shape
    split_view = values.reshape(n_rows // dilation, dilation, n_heads // dilation, dilation)
    return jnp.stack([split_view[:, residue, :, residue] for residue in range(dilation)], axis=2)


def place_rows(picked, dilation):
    eye_f = jnp.eye(dilation, dtype=picked.dtype)
    spread = picked[:, None] * eye_f[None, :, None, :, None]
    return spread.reshape(picked.shape[0] * dilation, -1)


def place_stats(picked, dilation):
    eye_b = jnp.eye(dilation, dtype=bool)
    spread = jnp.where(eye_b[None, :, None, :], picked[:, None], -jnp.inf)
    return spread.reshape(picked.shape[0] * dilation, -1)


def branch_forward(q_blk, k_blk, v_blk):
    logits = jnp.einsum('siacd,sjacd->sacij', q_blk, k_blk, preferred_element_type=jnp.float32)
    row_max = jnp.max(logits, axis=-1, keepdims=True)
    exp_logits = jnp.exp(logits - row_max)
    row_sum = jnp.sum(exp_logits, axis=-1, keepdims=True)
    attn_probs = (exp_logits / row_sum).astype(jnp.bfloat16)
    seg_out = jnp.einsum('sacij,sjacd->siacd', attn_probs, v_blk, preferred_element_type=jnp.float32)
    seg_lse = jnp.transpose((row_max + jnp.log(row_sum))[..., 0], (0, 3, 1, 2))
    return seg_out, seg_lse


def branch_backward(q_blk, k_blk, v_blk, dout_blk, lse_blk, delta_blk):
    logits = jnp.einsum('siacd,sjacd->sacij', q_blk, k_blk, preferred_element_type=jnp.float32)
    attn_probs = jnp.exp(logits - jnp.transpose(lse_blk, (0, 2, 3, 1))[..., None])
    grad_v = jnp.einsum('sacij,siacd->sjacd', attn_probs.astype(jnp.bfloat16), dout_blk, preferred_element_type=jnp.float32)
    grad_p = jnp.einsum('siacd,sjacd->sacij', dout_blk, v_blk, preferred_element_type=jnp.float32)
    grad_s = (attn_probs * (grad_p - jnp.transpose(delta_blk, (0, 2, 3, 1))[..., None])).astype(jnp.bfloat16)
    grad_q = jnp.einsum('sacij,sjacd->siacd', grad_s, k_blk, preferred_element_type=jnp.float32) * HEAD_DIM ** -0.5
    grad_k = jnp.einsum('sacij,siacd->sjacd', grad_s, q_blk, preferred_element_type=jnp.float32)
    return grad_q, grad_k, grad_v


def solution(mesh):
    sp_size = mesh.shape['sp']
    q_scale = HEAD_DIM ** -0.5

    def gather_group(local_rows, group_size):
        pieces = [local_rows]
        for offset in range(1, group_size):
            perm_pairs = [(group_base + (member + offset) % group_size, group_base + member) for group_base in range(0, sp_size, group_size) for member in range(group_size)]
            pieces.append(lax.ppermute(local_rows, 'sp', perm_pairs))
        return jnp.concatenate(pieces, axis=0)

    def return_group(grad_rows, group_size):
        n_rows = grad_rows.shape[0] // group_size
        summed = grad_rows[:n_rows]
        for offset in range(1, group_size):
            perm_pairs = [(group_base + member, group_base + (member + offset) % group_size) for group_base in range(0, sp_size, group_size) for member in range(group_size)]
            summed = summed + lax.ppermute(grad_rows[offset * n_rows:(offset + 1) * n_rows], 'sp', perm_pairs)
        return summed

    def device_step(x_loc, w_q, w_k, w_v, w_o, dy_loc):
        tokens, model_dim = x_loc.shape
        n_heads = model_dim // HEAD_DIM
        q_rows = jnp.dot(x_loc, w_q, preferred_element_type=jnp.float32).astype(jnp.bfloat16) * q_scale
        k_rows = jnp.dot(x_loc, w_k, preferred_element_type=jnp.float32).astype(jnp.bfloat16)
        v_rows = jnp.dot(x_loc, w_v, preferred_element_type=jnp.float32).astype(jnp.bfloat16)
        saved_blocks = []
        branch_outs = []
        branch_lses = []
        for dilation in DILATIONS:
            seg_len = tokens * dilation // 2
            group_size = max(seg_len // tokens, 1)
            q_sel = pick_rows(q_rows, dilation)
            k_sel = pick_rows(k_rows, dilation)
            v_sel = pick_rows(v_rows, dilation)
            if group_size > 1:
                q_blk = q_sel[None]
                k_blk = gather_group(k_sel, group_size)[None]
                v_blk = gather_group(v_sel, group_size)[None]
            else:
                blk_shape = (tokens // seg_len, seg_len // dilation) + q_sel.shape[1:]
                q_blk = q_sel.reshape(blk_shape)
                k_blk = k_sel.reshape(blk_shape)
                v_blk = v_sel.reshape(blk_shape)
            seg_out, seg_lse = branch_forward(q_blk, k_blk, v_blk)
            branch_outs.append(place_rows(seg_out.reshape(q_sel.shape), dilation))
            branch_lses.append(place_stats(seg_lse.reshape(q_sel.shape[:-1]), dilation))
            saved_blocks.append((dilation, group_size, q_blk, k_blk, v_blk))
        lse_stack = jnp.stack(branch_lses)
        lse_max = jnp.max(lse_stack, axis=0)
        branch_w = jnp.exp(lse_stack - lse_max)
        norm_sum = jnp.sum(branch_w, axis=0)
        out_stack = jnp.stack(branch_outs).reshape(len(DILATIONS), tokens, n_heads, HEAD_DIM)
        attn_out = jnp.sum(branch_w[..., None] * out_stack, axis=0) / norm_sum[..., None]
        lse_all = lse_max + jnp.log(norm_sum)
        attn_b = attn_out.reshape(tokens, model_dim).astype(jnp.bfloat16)
        y_loc = jnp.dot(attn_b, w_o, preferred_element_type=jnp.float32).astype(jnp.bfloat16)
        dw_o = jnp.einsum('td,te->de', attn_b, dy_loc, preferred_element_type=jnp.float32)
        d_attn = jnp.einsum('te,de->td', dy_loc, w_o, preferred_element_type=jnp.float32).astype(jnp.bfloat16)
        row_delta = jnp.sum(d_attn.reshape(tokens, n_heads, HEAD_DIM).astype(jnp.float32) * attn_out, axis=-1)
        dq_acc = jnp.zeros((tokens, model_dim), jnp.float32)
        dk_acc = dq_acc
        dv_acc = dq_acc
        for dilation, group_size, q_blk, k_blk, v_blk in saved_blocks:
            stat_shape = q_blk.shape[:-1]
            dout_blk = pick_rows(d_attn, dilation).reshape(q_blk.shape)
            lse_blk = pick_stats(lse_all, dilation).reshape(stat_shape)
            delta_blk = pick_stats(row_delta, dilation).reshape(stat_shape)
            grad_q, grad_k, grad_v = branch_backward(q_blk, k_blk, v_blk, dout_blk, lse_blk, delta_blk)
            sel_shape = (tokens // dilation,) + q_blk.shape[2:]
            if group_size > 1:
                grad_k = return_group(grad_k[0], group_size)
                grad_v = return_group(grad_v[0], group_size)
            dq_acc = dq_acc + place_rows(grad_q.reshape(sel_shape), dilation)
            dk_acc = dk_acc + place_rows(grad_k.reshape(sel_shape), dilation)
            dv_acc = dv_acc + place_rows(grad_v.reshape(sel_shape), dilation)
        dq_b = dq_acc.astype(jnp.bfloat16)
        dk_b = dk_acc.astype(jnp.bfloat16)
        dv_b = dv_acc.astype(jnp.bfloat16)
        dx_sum = jnp.einsum('td,ed->te', dq_b, w_q, preferred_element_type=jnp.float32) + jnp.einsum('td,ed->te', dk_b, w_k, preferred_element_type=jnp.float32) + jnp.einsum('td,ed->te', dv_b, w_v, preferred_element_type=jnp.float32)
        dx_loc = dx_sum.astype(jnp.bfloat16)
        dw_q = jnp.einsum('td,te->de', x_loc, dq_b, preferred_element_type=jnp.float32)
        dw_k = jnp.einsum('td,te->de', x_loc, dk_b, preferred_element_type=jnp.float32)
        dw_v = jnp.einsum('td,te->de', x_loc, dv_b, preferred_element_type=jnp.float32)
        dw_q, dw_k, dw_v, dw_o = lax.psum((dw_q, dw_k, dw_v, dw_o), 'sp')
        return y_loc, dx_loc, dw_q, dw_k, dw_v, dw_o

    row_spec = P(('dp', 'sp'), None)
    full_spec = P(None, None)
    grad_spec = P('dp', None)
    return jax.shard_map(device_step, mesh=mesh, in_specs=(row_spec, full_spec, full_spec, full_spec, full_spec, row_spec), out_specs=(row_spec, row_spec, grad_spec, grad_spec, grad_spec, grad_spec), check_vma=False)
```

profile of v0, /device:TPU:0, one launch (start us, length us, event | category | flops | bytes accessed | tf_op | source)
XLA Modules:
  0.0 1153.2 jit_solution(17151026045560450572)
XLA Ops:
  52.8 7.1 reshape.879
  59.9 6.9 reshape.878
  72.1 6.6 reshape.874
  78.7 6.9 reshape.872
  101.1 6.6 reshape.873
  107.7 7.1 reshape.871
  129.7 6.6 reshape.887
  136.3 7.0 reshape.883
  151.5 5.6 fusion.76
  164.1 5.8 fusion.75
  212.2 5.4 copy.1307
  217.6 11.0 fusion.86
  228.6 9.8 fusion
  274.5 5.6 fusion.74
  340.8 5.6 fusion.71
  360.6 6.6 fusion.32
  367.2 5.4 copy.1346
  372.7 6.7 mul.335
  379.4 6.5 copy.1347
  386.5 9.1 fusion.21
  399.8 5.6 stack.72
  436.4 6.9 copy.1363
  479.0 6.6 copy.1353
  517.0 7.0 maximum_add_fusion
  525.4 6.8 fusion.25
  540.2 11.5 fusion.22
  551.7 14.8 %multiply_convert_fusion = bf16[2,16,384,384]{2,3,1,0:T(8,128)(2,1)} fusion(f32[2,16,384,384]{2,3,1,0:T(8,128)} %get-tuple-element.186, f32[2,16,384]{2,1,0:T(8,128)S(1)} %copy.1372, f32[2,16,384]{2,1,0:T(8,128)S(1)} %fusion.50, bf16[2,384,16,64]{1,3,2,0:T(8,128)(2,1)} %copy.1369, bf16[2,384,16,64]{1,3,2,0:T(8,128)(2,1)} %copy.1340), kind=kOutput, calls=%fused_computation | convolution fusion | flops 622854144 | bytes 31555584 | tf_op jit(solution)/shard_map/siacd,sjacd->sacij/dot_general | solution.py:50
  566.4 9.3 convolution_bitcast_fusion.3
  609.4 5.4 copy.1384
  614.8 5.3 copy.1417
  620.1 5.3 copy.1427
  625.4 15.4 %broadcast_multiply_fusion.2 = (f32[384,2,8,2,64]{4,3,2,1,0:T(2,128)}, f32[384,2,8,2,64]{4,3,2,1,0:T(2,128)}, f32[384,2,8,2,64]{4,3,2,1,0:T(2,128)}) fusion(f32[384,8,2,64]{3,2,1,0:T(2,128)} %copy.1427, f32[2,2]{1,0:T(2,128)S(1)} %copy-done.137, f32[384,8,2,64]{3,2,1,0:T(2,128)} %copy.1417, f32[384,8,2,64]{3,2,1,0:T(2,128)} %copy.1384), kind=kLoop, calls=%fused_computation.30 | loop fusion | flops 2359296 | bytes 14155792 | tf_op jit(solution)/shard_map/mul | solution.py:25
  669.7 8.4 mul.405
  681.6 8.5 mul.395
  693.7 8.4 mul.371
  714.9 8.9 broadcast_multiply_fusion
  723.8 6.3 mul.411
  733.7 6.3 mul.401
  743.5 6.3 mul.391
  759.9 9.7 broadcast_multiply_fusion.1
  769.6 7.3 mul.408
  780.4 7.3 mul.398
  791.3 7.3 mul.381
  802.3 5.5 add_convert_fusion.2
  838.4 286.7 %all-reduce.3.cloned.1.call-done = (f32[1024,1024]{0,1:T(8,128)}, f32[1024,1024]{0,1:T(8,128)}, f32[1024,1024]{0,1:T(8,128)}, f32[1024,1024]{1,0:T(8,128)}) async-done(((f32[1024,1024]{0,1:T(8,128)}, f32[1024,1024]{0,1:T(8,128)}, f32[1024,1024]{0,1:T(8,128)}, f32[1024,1024]{1,0:T(8,128)}), (f32[1024,1024]{0,1:T(8,128)}, f32[1024,1024]{0,1:T(8,128)}, f32[1024,1024]{0,1:T(8,128)}, ...) | async-done | bytes 16777232 | tf_op jit(solution)/shard_map/psum | solution.py:140
  1125.1 5.3 copy.1433
  1130.4 5.3 copy.1434
  1135.7 5.3 copy.1435
  (619 shorter events, 505.7 us)
Async XLA Ops:
  7.2 112.9 %copy-start = (bf16[1024,1024]{1,0:T(8,128)(2,1)S(1)}, bf16[1024,1024]{1,0:T(8,128)(2,1)}, u32[]{:S(2)}) copy-start(bf16[1024,1024]{1,0:T(8,128)(2,1)} %param.10) | copy-start | bytes 6291460
  7.2 1117.9 %all-reduce.3.cloned.1.call-start = ((), (), s32[]{:S(2)}) async-start(), calls=%async_computation | async-start | bytes 33554432 | tf_op jit(solution)/shard_map/psum | solution.py:140
  26.1 398.4 %collective-permute-start.7 = (bf16[96,2,8,64]{0,3,2,1:T(8,128)(2,1)}, bf16[96,2,8,64]{0,3,2,1:T(8,128)(2,1)}, u32[]{:S(2)}, u32[]{:S(2)}) collective-permute-start(bf16[96,2,8,64]{0,3,2,1:T(8,128)(2,1)} %constant_dynamic-update-slice_fusion.16), channel_id=1, source_target_pairs={{3,0},{0,1},{1,2},{2,3},{7,4},{4,5},{5,6},{6,7},{11,8},{8,9},{9,10... | collective-permute-start | bytes 589832 | tf_op jit(solution)/shard_map/ppermute | solution.py:65
  26.6 397.9 %collective-permute-start.6 = (bf16[96,2,8,64]{0,3,2,1:T(8,128)(2,1)}, bf16[96,2,8,64]{0,3,2,1:T(8,128)(2,1)}, u32[]{:S(2)}, u32[]{:S(2)}) collective-permute-start(bf16[96,2,8,64]{0,3,2,1:T(8,128)(2,1)} %constant_dynamic-update-slice_fusion.16), channel_id=1, source_target_pairs={{2,0},{3,1},{0,2},{1,3},{6,4},{7,5},{4,6},{5,7},{10,8},{11,9},{8,1... | collective-permute-start | bytes 589832 | tf_op jit(solution)/shard_map/ppermute | solution.py:65
  47.9 363.9 %collective-permute-start.3 = (bf16[96,2,8,64]{0,3,2,1:T(8,128)(2,1)}, bf16[96,2,8,64]{0,3,2,1:T(8,128)(2,1)}, u32[]{:S(2)}, u32[]{:S(2)}) collective-permute-start(bf16[96,2,8,64]{0,3,2,1:T(8,128)(2,1)} %constant_dynamic-update-slice_fusion.8), channel_id=1, source_target_pairs={{3,0},{0,1},{1,2},{2,3},{7,4},{4,5},{5,6},{6,7},{11,8},{8,9},{9,10... | collective-permute-start | bytes 589832 | tf_op jit(solution)/shard_map/ppermute | solution.py:65
  48.0 364.2 %collective-permute-start.2 = (bf16[96,2,8,64]{0,3,2,1:T(8,128)(2,1)}, bf16[96,2,8,64]{0,3,2,1:T(8,128)(2,1)}, u32[]{:S(2)}, u32[]{:S(2)}) collective-permute-start(bf16[96,2,8,64]{0,3,2,1:T(8,128)(2,1)} %constant_dynamic-update-slice_fusion.8), channel_id=1, source_target_pairs={{2,0},{3,1},{0,2},{1,3},{6,4},{7,5},{4,6},{5,7},{10,8},{11,9},{8,1... | collective-permute-start | bytes 589832 | tf_op jit(solution)/shard_map/ppermute | solution.py:65
  49.7 362.7 %collective-permute-start.1 = (bf16[96,2,8,64]{0,3,2,1:T(8,128)(2,1)}, bf16[96,2,8,64]{0,3,2,1:T(8,128)(2,1)}, u32[]{:S(2)}, u32[]{:S(2)}) collective-permute-start(bf16[96,2,8,64]{0,3,2,1:T(8,128)(2,1)} %constant_dynamic-update-slice_fusion.8), channel_id=1, source_target_pairs={{1,0},{2,1},{3,2},{0,3},{5,4},{6,5},{7,6},{4,7},{9,8},{10,9},{11,1... | collective-permute-start | bytes 589832 | tf_op jit(solution)/shard_map/ppermute | solution.py:65
  49.7 201.0 %copy-start.134 = (pred[4,4]{0,1:T(4,128)(4,1)}, pred[4,4]{0,1:T(4,128)(4,1)S(1)}, u32[]{:S(2)}) copy-start(pred[4,4]{0,1:T(4,128)(4,1)S(1)} %iota_compare_fusion.1) | copy-start | bytes 52
  49.7 134.6 %copy-start.138 = (pred[2,2]{0,1:T(4,128)(4,1)}, pred[2,2]{0,1:T(4,128)(4,1)S(1)}, u32[]{:S(2)}) copy-start(pred[2,2]{0,1:T(4,128)(4,1)S(1)} %iota_compare_fusion.2) | copy-start | bytes 16
  49.8 10.1 copy-start.131
  164.1 14.2 %copy-start.32 = (bf16[384,1,8,1,64]{0,4,2,3,1:T(8,128)(2,1)}, bf16[384,1,8,1,64]{0,4,2,3,1:T(8,128)(2,1)S(1)}, u32[]{:S(2)}) copy-start(bf16[384,1,8,1,64]{0,4,2,3,1:T(8,128)(2,1)S(1)} %copy.1457) | copy-start | bytes 1179652
  173.4 7.4 copy-start.34
  411.7 12.7 %collective-permute-start.5 = (bf16[96,2,8,64]{0,3,2,1:T(8,128)(2,1)}, bf16[96,2,8,64]{0,3,2,1:T(8,128)(2,1)}, u32[]{:S(2)}, u32[]{:S(2)}) collective-permute-start(bf16[96,2,8,64]{0,3,2,1:T(8,128)(2,1)} %constant_dynamic-update-slice_fusion.16), channel_id=1, source_target_pairs={{1,0},{2,1},{3,2},{0,3},{5,4},{6,5},{7,6},{4,7},{9,8},{10,9},{11,1... | collective-permute-start | bytes 589832 | tf_op jit(solution)/shard_map/ppermute | solution.py:65
  412.2 54.3 %collective-permute-start.4 = (bf16[192,4,4,64]{0,3,2,1:T(8,128)(2,1)}, bf16[192,4,4,64]{0,3,2,1:T(8,128)(2,1)}, u32[]{:S(2)}, u32[]{:S(2)}) collective-permute-start(bf16[192,4,4,64]{0,3,2,1:T(8,128)(2,1)} %pad_maximum_fusion.10), channel_id=1, source_target_pairs={{1,0},{0,1},{3,2},{2,3},{5,4},{4,5},{7,6},{6,7},{9,8},{8,9},{11,10... | collective-permute-start | bytes 1179656 | tf_op jit(solution)/shard_map/ppermute | solution.py:65
  412.4 30.9 %collective-permute-start = (bf16[192,4,4,64]{0,3,2,1:T(8,128)(2,1)}, bf16[192,4,4,64]{0,3,2,1:T(8,128)(2,1)}, u32[]{:S(2)}, u32[]{:S(2)}) collective-permute-start(bf16[192,4,4,64]{0,3,2,1:T(8,128)(2,1)} %pad_maximum_fusion.9), channel_id=1, source_target_pairs={{1,0},{0,1},{3,2},{2,3},{5,4},{4,5},{7,6},{6,7},{9,8},{8,9},{11,10... | collective-permute-start | bytes 1179656 | tf_op jit(solution)/shard_map/ppermute | solution.py:65
  417.7 12.1 %copy-start.98 = (f32[96,2,8]{0,2,1:T(8,128)}, f32[96,2,8]{0,2,1:T(8,128)S(1)}, u32[]{:S(2)}) copy-start(f32[96,2,8]{0,2,1:T(8,128)S(1)} %add_bitcast_fusion.3) | copy-start | bytes 18436
  436.3 6.9 copy-start.61
  436.3 6.9 copy-start.63
  436.3 6.9 copy-start.65
  436.3 6.9 copy-start.67
  436.3 6.9 copy-start.70
  436.4 6.9 copy-start.73
  458.2 8.3 copy-start.80
  458.2 8.3 copy-start.83
  458.2 8.3 copy-start.86
  479.0 6.7 copy-start.101
  516.9 15.3 %slice-start = ((s8[9437184]{0:T(1024)(128)(4,1)}), s8[4194304]{0:T(1024)(128)(4,1)S(1)}, s32[]{:S(2)}) async-start(s8[9437184]{0:T(1024)(128)(4,1)} %bitcast.503), calls=%async_computation.1 | async-start | bytes 8388608
  516.9 15.3 %slice-start.1 = ((s8[9437184]{0:T(1024)(128)(4,1)}), s8[4194304]{0:T(1024)(128)(4,1)S(1)}, s32[]{:S(2)}) async-start(s8[9437184]{0:T(1024)(128)(4,1)} %bitcast.503), calls=%async_computation.2 | async-start | bytes 8388608
  525.4 6.9 slice-start.2
  525.4 6.8 copy-start.54
  525.4 6.8 copy-start.56
  566.4 9.4 copy-start.2
  566.4 9.4 copy-start.5
  589.1 56.2 %collective-permute-start.13 = (f32[96,2,8,64]{0,3,2,1:T(8,128)}, f32[96,2,8,64]{0,3,2,1:T(8,128)}, u32[]{:S(2)}, u32[]{:S(2)}) collective-permute-start(f32[96,2,8,64]{0,3,2,1:T(8,128)} %get-tuple-element.164), channel_id=1, source_target_pairs={{0,1},{1,2},{2,3},{3,0},{4,5},{5,6},{6,7},{7,4},{8,9},{9,10},{10,1... | collective-permute-start | bytes 1179656 | tf_op jit(solution)/shard_map/ppermute | solution.py:73
  589.3 116.3 %collective-permute-start.15 = (f32[96,2,8,64]{0,3,2,1:T(8,128)}, f32[96,2,8,64]{0,3,2,1:T(8,128)}, u32[]{:S(2)}, u32[]{:S(2)}) collective-permute-start(f32[96,2,8,64]{0,3,2,1:T(8,128)} %get-tuple-element.165), channel_id=1, source_target_pairs={{0,3},{1,0},{2,1},{3,2},{4,7},{5,4},{6,5},{7,6},{8,11},{9,8},{10,9... | collective-permute-start | bytes 1179656 | tf_op jit(solution)/shard_map/ppermute | solution.py:73
  590.9 116.3 %collective-permute-start.14 = (f32[96,2,8,64]{0,3,2,1:T(8,128)}, f32[96,2,8,64]{0,3,2,1:T(8,128)}, u32[]{:S(2)}, u32[]{:S(2)}) collective-permute-start(f32[96,2,8,64]{0,3,2,1:T(8,128)} %get-tuple-element.166), channel_id=1, source_target_pairs={{0,2},{1,3},{2,0},{3,1},{4,6},{5,7},{6,4},{7,5},{8,10},{9,11},{10,... | collective-permute-start | bytes 1179656 | tf_op jit(solution)/shard_map/ppermute | solution.py:73
  604.8 104.2 %collective-permute-start.11 = (f32[96,2,8,64]{0,3,2,1:T(8,128)}, f32[96,2,8,64]{0,3,2,1:T(8,128)}, u32[]{:S(2)}, u32[]{:S(2)}) collective-permute-start(f32[96,2,8,64]{0,3,2,1:T(8,128)} %get-tuple-element.168), channel_id=1, source_target_pairs={{0,3},{1,0},{2,1},{3,2},{4,7},{5,4},{6,5},{7,6},{8,11},{9,8},{10,9... | collective-permute-start | bytes 1179656 | tf_op jit(solution)/shard_map/ppermute | solution.py:73
  625.3 15.4 %copy-start.23 = (f32[1,384,4,4,64]{1,4,3,2,0:T(8,128)S(1)}, f32[1,384,4,4,64]{1,4,3,2,0:T(8,128)}, u32[]{:S(2)}) copy-start(f32[1,384,4,4,64]{1,4,3,2,0:T(8,128)} %convolution_bitcast_fusion.4) | copy-start | bytes 4718596
  625.4 16.7 %copy-start.31 = (bf16[4,4,192,384]{3,2,1,0:T(8,128)(2,1)S(1)}, bf16[4,4,192,384]{3,2,1,0:T(8,128)(2,1)}, u32[]{:S(2)}) copy-start(bf16[4,4,192,384]{3,2,1,0:T(8,128)(2,1)} %copy-done.30) | copy-start | bytes 7077892
  625.4 16.7 %copy-start.71 = (bf16[192,1,4,1,64]{0,4,2,3,1:T(8,128)(2,1)S(1)}, bf16[192,1,4,1,64]{0,4,2,3,1:T(8,128)(2,1)}, u32[]{:S(2)}) copy-start(bf16[192,1,4,1,64]{0,4,2,3,1:T(8,128)(2,1)} %copy.1462) | copy-start | bytes 294916
  625.4 16.7 %copy-start.74 = (bf16[192,1,4,1,64]{0,4,2,3,1:T(8,128)(2,1)S(1)}, bf16[192,1,4,1,64]{0,4,2,3,1:T(8,128)(2,1)}, u32[]{:S(2)}) copy-start(bf16[192,1,4,1,64]{0,4,2,3,1:T(8,128)(2,1)} %copy.1464) | copy-start | bytes 294916
  625.4 16.7 %copy-start.76 = (bf16[192,1,4,1,64]{0,4,2,3,1:T(8,128)(2,1)S(1)}, bf16[192,1,4,1,64]{0,4,2,3,1:T(8,128)(2,1)}, u32[]{:S(2)}) copy-start(bf16[192,1,4,1,64]{0,4,2,3,1:T(8,128)(2,1)} %copy.1463) | copy-start | bytes 294916
  625.4 16.7 %copy-start.78 = (bf16[192,1,4,1,64]{0,4,2,3,1:T(8,128)(2,1)S(1)}, bf16[192,1,4,1,64]{0,4,2,3,1:T(8,128)(2,1)}, u32[]{:S(2)}) copy-start(bf16[192,1,4,1,64]{0,4,2,3,1:T(8,128)(2,1)} %copy.1465) | copy-start | bytes 294916
  642.1 66.8 %collective-permute-start.9 = (f32[96,2,8,64]{0,3,2,1:T(8,128)}, f32[96,2,8,64]{0,3,2,1:T(8,128)}, u32[]{:S(2)}, u32[]{:S(2)}) collective-permute-start(f32[96,2,8,64]{0,3,2,1:T(8,128)} %get-tuple-element.167), channel_id=1, source_target_pairs={{0,1},{1,2},{2,3},{3,0},{4,5},{5,6},{6,7},{7,4},{8,9},{9,10},{10,1... | collective-permute-start | bytes 1179656 | tf_op jit(solution)/shard_map/ppermute | solution.py:73
  645.3 63.6 %collective-permute-start.10 = (f32[96,2,8,64]{0,3,2,1:T(8,128)}, f32[96,2,8,64]{0,3,2,1:T(8,128)}, u32[]{:S(2)}, u32[]{:S(2)}) collective-permute-start(f32[96,2,8,64]{0,3,2,1:T(8,128)} %get-tuple-element.169), channel_id=1, source_target_pairs={{0,2},{1,3},{2,0},{3,1},{4,6},{5,7},{6,4},{7,5},{8,10},{9,11},{10,... | collective-permute-start | bytes 1179656 | tf_op jit(solution)/shard_map/ppermute | solution.py:73
  705.6 47.8 %collective-permute-start.12 = (f32[192,4,4,64]{0,3,2,1:T(8,128)}, f32[192,4,4,64]{0,3,2,1:T(8,128)}, u32[]{:S(2)}, u32[]{:S(2)}) collective-permute-start(f32[192,4,4,64]{0,3,2,1:T(8,128)} %slice_bitcast_fusion), channel_id=1, source_target_pairs={{0,1},{1,0},{2,3},{3,2},{4,5},{5,4},{6,7},{7,6},{8,9},{9,8},{10,11... | collective-permute-start | bytes 2359304 | tf_op jit(solution)/shard_map/ppermute | solution.py:73
  707.2 49.4 %collective-permute-start.8 = (f32[192,4,4,64]{0,3,2,1:T(8,128)}, f32[192,4,4,64]{0,3,2,1:T(8,128)}, u32[]{:S(2)}, u32[]{:S(2)}) collective-permute-start(f32[192,4,4,64]{0,3,2,1:T(8,128)} %slice_bitcast_fusion.2), channel_id=1, source_target_pairs={{0,1},{1,0},{2,3},{3,2},{4,5},{5,4},{6,7},{7,6},{8,9},{9,8},{10,11... | collective-permute-start | bytes 2359304 | tf_op jit(solution)/shard_map/ppermute | solution.py:73
  802.3 9.5 copy-start.15
  (119 other events, 430.5 us)
Sparse Core Ops, SparseCore 0:
  826.5 298.5 all-reduce.2
where the time goes:
time: 1170 us; the launch traced here: 1150 us
  local copies, waits for them, and re-layouts  591 us (51%)
  waiting for transfers between devices  287 us (25%)
  matrix products  158 us (14%)
  other arithmetic  89.6 us (8%)
  between operations  16.9 us (1%)
    psum x1, waiting for transfers between devices, device_step(): dw_q, dw_k, dw_v, dw_o = lax.psum((dw_q, dw_k, dw_v, dw_o), 'sp')  287 us
    mul x38, local copies, waits for them, and re-layouts, place_rows(): spread = picked[:, None] * eye_f[None, :, None, :, None]  175 us
    unnamed x406, local copies, waits for them, and re-layouts  124 us
    reshape x12, local copies, waits for them, and re-layouts, pick_rows(): values.reshape(n_rows // dilation, dilation, groups, dilation, HEAD_DIM)  75.7 us
    slice x12, local copies, waits for them, and re-layouts, pick_rows(): split_view[:, residue, :, residue, :]  50.5 us
    mul x5, other arithmetic, place_rows(): spread = picked[:, None] * eye_f[None, :, None, :, None]  41.5 us
    another operation x8, local copies, waits for them, and re-layouts  41.3 us
    select_n x12, local copies, waits for them, and re-layouts, place_stats(): spread = jnp.where(eye_b[None, :, None, :], picked[:, None], -jnp.inf)  34 us
  transfers between devices with their start and end apart: 17, of which 1 were waited for; matrix products, arithmetic and copies ran while one was open for 52% of the time, Pallas kernels for 0%

commit v1 on v0

v1 whole, which is shorter than its diff:
```python
import functools

import jax
import jax.numpy as jnp
from jax import lax
from jax.experimental import pallas as pl
from jax.experimental.pallas import tpu as pltpu
from jax.sharding import PartitionSpec as P

BF = jnp.bfloat16
F32 = jnp.float32
T = 768
D = 1024
CH = 96
NK = 384
ORDER = (0, 4, 2, 6, 1, 5, 3, 7)
NT = (((1,), (1,)), ((), ()))


def dot(a, b):
    return jnp.dot(a, b, preferred_element_type=F32)


def dot_nt(a, b):
    return lax.dot_general(a, b, NT, preferred_element_type=F32)


def perm_matrix(inverse):
    a = lax.broadcasted_iota(jnp.int32, (128, 128), 1 if inverse else 0)
    b = lax.broadcasted_iota(jnp.int32, (128, 128), 0 if inverse else 1)
    c = a // 16
    res = 4 * (c % 2) + 2 * ((c // 2) % 2) + c // 4
    src = (a % 16) * 8 + res
    return jnp.where(src == b, 1.0, 0.0).astype(BF)


def permute_into(src_ref, dst_ref):
    m = perm_matrix(False)
    for blk in range(T // 128):
        z = dot(m, src_ref[blk * 128:(blk + 1) * 128, :]).astype(BF)
        for c in range(8):
            dst_ref[c * CH + blk * 16:c * CH + blk * 16 + 16, :] = z[c * 16:c * 16 + 16, :]


def unpermute_into(src_ref, dst_ref):
    m = perm_matrix(True)
    for blk in range(T // 128):
        z = jnp.concatenate([src_ref[c * CH + blk * 16:c * CH + blk * 16 + 16, :] for c in range(8)], axis=0)
        dst_ref[blk * 128:(blk + 1) * 128, :] = dot(m, z).astype(BF)


def starts(p):
    return 2 * (p % 2), 2 * (p % 2) + (p // 2) % 2


def left_lanes(n):
    return lax.broadcasted_iota(jnp.int32, (n, 128), 1) < 64


def project_kernel(x_ref, dy_ref, wq_ref, wk_ref, wv_ref, wo_ref, xp_ref, xt_ref, dyp_ref, q_ref, k_ref, v_ref, do_ref, sel_ref):
    j = pl.program_id(0)

    @pl.when(j == 0)
    def _():
        permute_into(x_ref, xp_ref)
        permute_into(dy_ref, dyp_ref)
        for i in range(8):
            xt_ref[128 * i:128 * i + 128, :] = xp_ref[:, 128 * i:128 * i + 128].T

    q_ref[...] = (dot(xp_ref[...], wq_ref[...]).astype(BF) * 0.125).astype(BF)
    k_ref[...] = dot(xp_ref[...], wk_ref[...]).astype(BF)
    v_ref[...] = dot(xp_ref[...], wv_ref[...]).astype(BF)
    do_ref[...] = dot_nt(dyp_ref[...], wo_ref[...]).astype(BF)
    for i in range(2):
        s4, s8 = starts(2 * j + i)
        cols = slice(128 * i, 128 * i + 128)
        for which, src in enumerate((k_ref, v_ref)):
            for first, n, at in ((s4, 192, 0), (s8, 96, 192)):
                even = src[pl.ds(pl.multiple_of(first * CH, CH), n), cols]
                odd = src[pl.ds(pl.multiple_of(first * CH + NK, CH), n), cols]
                sel_ref[which, at:at + n, cols] = jnp.where(left_lanes(n), even, odd)


def project(x, dy, wq, wk, wv, wo):
    full = pl.BlockSpec((T, D), lambda j: (0, 0))
    wcol = pl.BlockSpec((D, 256), lambda j: (0, j))
    wrow = pl.BlockSpec((256, D), lambda j: (j, 0))
    tcol = pl.BlockSpec((T, 256), lambda j: (0, j))
    tok = jax.ShapeDtypeStruct((T, D), BF)
    return pl.pallas_call(
        project_kernel, grid=(4,), name='project',
        in_specs=[full, full, wcol, wcol, wcol, wrow],
        out_specs=[full, pl.BlockSpec((D, T), lambda j: (0, 0)), full, tcol, tcol, tcol, tcol, pl.BlockSpec((2, 288, 256), lambda j: (0, 0, j))],
        out_shape=[tok, jax.ShapeDtypeStruct((D, T), BF), tok, tok, tok, tok, tok, jax.ShapeDtypeStruct((2, 288, D), BF)],
        compiler_params=pltpu.CompilerParams(vmem_limit_bytes=56 << 20),
        cost_estimate=pl.CostEstimate(flops=6_500_000_000, bytes_accessed=24_000_000, transcendentals=0),
    )(x, dy, wq, wk, wv, wo)


def attention_kernel(q_ref, k_ref, v_ref, do_ref, h1_ref, h2_ref, h3_ref,
                     at_ref, dq_ref, dk_ref, dv_ref, r1_ref, r2_ref, r3_ref,
                     e_ref, m_ref, acc_ref, dqa_ref, de_ref):
    p = pl.program_id(0)
    s4, s8 = starts(p)
    left = left_lanes(NK)

    def rows_of(ref, first, n):
        return ref[pl.ds(first, n // CH)].reshape(n, ref.shape[-1])

    def pick(ref, b):
        if b < 2:
            return ref[:, b].reshape(NK, 128)
        first, n = BLOCKS[b]
        return jnp.where(left[:n], rows_of(ref, first, n), rows_of(ref, first + 4, n))

    BLOCKS = {0: (None, NK), 1: (None, NK), 2: (0, NK), 3: (s4, 192), 4: (s8, 96)}
    OFFS = (0, 384, 768, 1152, 1344)

    def keys(ref, which, b):
        own = pick(ref, b)
        if b < 3:
            return own
        if b == 3:
            return jnp.concatenate([own, h1_ref[which, 0:192, :]], axis=0)
        return jnp.concatenate([own, h1_ref[which, 192:288, :], h2_ref[which], h3_ref[which]], axis=0)

    def get(ref, e, b):
        w = ref.shape[-1]
        if b < 2:
            return ref[e, :, b].reshape(NK, w)
        first, n = BLOCKS[b]
        return ref[e, pl.ds(first + 4 * e, n // CH)].reshape(n, w)

    def put(ref, e, b, val):
        w = ref.shape[-1]
        if b < 2:
            ref[e, :, b] = val.reshape(8, 48, w)
        else:
            first, n = BLOCKS[b]
            ref[e, pl.ds(first + 4 * e, n // CH)] = val.reshape(n // CH, 2, 48, w)

    def head(val, e):
        keep = left[:val.shape[0]] if e == 0 else jnp.logical_not(left[:val.shape[0]])
        return jnp.where(keep, val, jnp.zeros_like(val))

    def wide(val):
        return jnp.concatenate([val, val, val], axis=1)

    for b in range(5):
        n = BLOCKS[b][1]
        qs, ks = pick(q_ref, b), keys(k_ref, 0, b)
        for e in range(2):
            s = dot_nt(head(qs, e), ks)
            e_ref[e, OFFS[b]:OFFS[b] + n, :] = s
            mx = jnp.broadcast_to(jnp.max(s, axis=1, keepdims=True), (n, 128))
            if b >= 2:
                mx = jnp.maximum(mx, get(m_ref, e, b))
            put(m_ref, e, b, mx)
    ones = jnp.ones((NK, 128), BF)
    for b in range(5):
        n = BLOCKS[b][1]
        vo = jnp.concatenate([keys(v_ref, 1, b), ones], axis=1)
        for e in range(2):
            ex = jnp.exp(e_ref[e, OFFS[b]:OFFS[b] + n, :] - wide(get(m_ref, e, b)))
            e_ref[e, OFFS[b]:OFFS[b] + n, :] = ex
            o = dot(ex.astype(BF), vo)
            if b >= 2:
                o = o + get(acc_ref, e, b)
            put(acc_ref, e, b, o)
    for c in range(8):
        outs = []
        dd = do_ref[c].reshape(CH, 128).astype(F32)
        for e in range(2):
            acc = acc_ref[e, c].reshape(CH, 256)
            linv = 1.0 / acc[:, 128:]
            o = acc[:, :128] * linv
            outs.append(o)
            de = jnp.sum(head(dd * o, e), axis=1, keepdims=True)
            m_ref[e, c] = linv.reshape(2, 48, 128)
            de_ref[e, c] = jnp.broadcast_to(de, (CH, 128)).reshape(2, 48, 128)
        at_ref[c] = jnp.where(left[:CH], outs[0], outs[1]).astype(BF).reshape(2, 48, 128)
    for b in range(5):
        n = BLOCKS[b][1]
        qs, ks, dos, vs = pick(q_ref, b), keys(k_ref, 0, b), pick(do_ref, b), keys(v_ref, 1, b)
        qt, dot_t = qs.T, dos.T
        dkt, dvt = [], []
        for e in range(2):
            half = slice(64 * e, 64 * e + 64)
            pn = e_ref[e, OFFS[b]:OFFS[b] + n, :] * wide(get(m_ref, e, b))
            dp = dot_nt(head(dos, e), vs)
            ds = (pn * (dp - wide(get(de_ref, e, b)))).astype(BF)
            dvt.append(dot(dot_t[half], pn.astype(BF)))
            dkt.append(dot(qt[half], ds))
            dq = dot(ds, ks)
            if b >= 2:
                dq = dq + get(dqa_ref, e, b)
            put(dqa_ref, e, b, dq)
        for which, (parts, own_ref) in enumerate(((dkt, dk_ref), (dvt, dv_ref))):
            g = jnp.concatenate(parts, axis=0).T
            if b < 2:
                own_ref[:, b] = g.reshape(8, 48, 128)
                continue
            first = BLOCKS[b][0]
            own = g[:n]
            zero = jnp.zeros_like(own)
            c = n // CH
            shape = (c, 2, 48, 128)
            own_ref[pl.ds(first, c)] += jnp.where(left[:n], own, zero).reshape(shape)
            own_ref[pl.ds(first + 4, c)] += jnp.where(left[:n], zero, own).reshape(shape)
            if b == 3:
                r1_ref[which, 0:192, :] = g[192:]
            if b == 4:
                r1_ref[which, 192:288, :] = g[96:192]
                r2_ref[which] = g[192:288]
                r3_ref[which] = g[288:384]
    for c in range(8):
        pair = jnp.where(left[:CH], dqa_ref[0, c].reshape(CH, 128), dqa_ref[1, c].reshape(CH, 128)) * 0.125
        dq_ref[c] = pair.astype(BF).reshape(2, 48, 128)


def attention(q, k, v, do, h1, h2, h3):
    heads = D // 128
    row = pl.BlockSpec((8, 2, 48, 128), lambda p: (0, 0, 0, p))
    big = pl.BlockSpec((2, 288, 128), lambda p: (0, 0, p))
    small = pl.BlockSpec((2, 96, 128), lambda p: (0, 0, p))
    r = lambda a: a.reshape(8, 2, 48, D)
    outs = pl.pallas_call(
        attention_kernel, grid=(heads,), name='attention',
        in_specs=[row] * 4 + [big, small, small],
        out_specs=[row] * 4 + [big, small, small],
        out_shape=[jax.ShapeDtypeStruct((8, 2, 48, D), BF)] * 2 + [jax.ShapeDtypeStruct((8, 2, 48, D), F32)] * 2
        + [jax.ShapeDtypeStruct((2, 288, D), F32)] + [jax.ShapeDtypeStruct((2, 96, D), F32)] * 2,
        scratch_shapes=[pltpu.VMEM((2, 1440, NK), F32), pltpu.VMEM((2, 8, 2, 48, 128), F32), pltpu.VMEM((2, 8, 2, 48, 256), F32),
                        pltpu.VMEM((2, 8, 2, 48, 128), F32), pltpu.VMEM((2, 8, 2, 48, 128), F32)],
        compiler_params=pltpu.CompilerParams(vmem_limit_bytes=56 << 20),
        cost_estimate=pl.CostEstimate(flops=30_000_000_000, bytes_accessed=24_000_000, transcendentals=9_000_000),
    )(r(q), r(k), r(v), r(do), h1, h2, h3)
    at, dq, dk, dv, r1, r2, r3 = outs
    f = lambda a: a.reshape(T, D)
    return f(at), f(dq), f(dk), f(dv), r1, r2, r3


def out_kernel(at_ref, att_ref, dyp_ref, wo_ref, xt_ref, dq_ref, y_ref, dwo_ref, dwq_ref, yp_ref):
    yp_ref[...] = dot(at_ref[...], wo_ref[...]).astype(BF)
    unpermute_into(yp_ref, y_ref)
    dwo_ref[...] = dot(att_ref[...].T, dyp_ref[...])
    dwq_ref[...] = dot(xt_ref[...], dq_ref[...])


def out_stage(at, dyp, wo, xt, dq):
    full = pl.BlockSpec((T, D), lambda j: (0, 0))
    col = pl.BlockSpec((D, 256), lambda j: (0, j))
    tcol = pl.BlockSpec((T, 256), lambda j: (0, j))
    return pl.pallas_call(
        out_kernel, grid=(4,), name='out_stage',
        in_specs=[full, tcol, full, col, pl.BlockSpec((D, T), lambda j: (0, 0)), tcol],
        out_specs=[tcol, pl.BlockSpec((256, D), lambda j: (j, 0)), col],
        out_shape=[jax.ShapeDtypeStruct((T, D), BF), jax.ShapeDtypeStruct((D, D), F32), jax.ShapeDtypeStruct((D, D), F32)],
        scratch_shapes=[pltpu.VMEM((T, 256), BF)],
        compiler_params=pltpu.CompilerParams(vmem_limit_bytes=56 << 20),
        cost_estimate=pl.CostEstimate(flops=5_000_000_000, bytes_accessed=20_000_000, transcendentals=0),
    )(at, at, dyp, wo, xt, dq)


def in_kernel(dq_ref, dk_ref, dv_ref, r1_ref, r2_ref, r3_ref, xt_ref, wq_ref, wk_ref, wv_ref, dx_ref, dwk_ref, dwv_ref, acc_ref, dxp_ref, sum_ref):
    j = pl.program_id(0)
    part = dot_nt(dq_ref[...], wq_ref[...])
    for which, (own_ref, w_ref, dw_ref) in enumerate(((dk_ref, wk_ref, dwk_ref), (dv_ref, wv_ref, dwv_ref))):
        sum_ref[...] = own_ref[...]
        for i in range(2):
            s4, s8 = starts(2 * j + i)
            cols = slice(128 * i, 128 * i + 128)
            a4 = r1_ref[which, 0:192, cols]
            a8 = r1_ref[which, 192:288, cols] + r2_ref[which, :, cols] + r3_ref[which, :, cols]
            for first, n, add in ((s4, 192, a4), (s8, 96, a8)):
                keep = left_lanes(n)
                zero = jnp.zeros_like(add)
                sum_ref[pl.ds(pl.multiple_of(first * CH, CH), n), cols] += jnp.where(keep, add, zero)
                sum_ref[pl.ds(pl.multiple_of(first * CH + NK, CH), n), cols] += jnp.where(keep, zero, add)
        g = sum_ref[...].astype(BF)
        dw_ref[...] = dot(xt_ref[...], g)
        part = part + dot_nt(g, w_ref[...])

    @pl.when(j == 0)
    def _():
        acc_ref[...] = part

    @pl.when(j > 0)
    def _():
        acc_ref[...] += part

    @pl.when(j == 3)
    def _():
        dxp_ref[...] = acc_ref[...].astype(BF)
        unpermute_into(dxp_ref, dx_ref)


def in_stage(dq, dk, dv, r1, r2, r3, xt, wq, wk, wv):
    full = pl.BlockSpec((T, D), lambda j: (0, 0))
    col = pl.BlockSpec((D, 256), lambda j: (0, j))
    tcol = pl.BlockSpec((T, 256), lambda j: (0, j))
    big = pl.BlockSpec((2, 288, 256), lambda j: (0, 0, j))
    small = pl.BlockSpec((2, 96, 256), lambda j: (0, 0, j))
    return pl.pallas_call(
        in_kernel, grid=(4,), name='in_stage',
        in_specs=[tcol, tcol, tcol, big, small, small, pl.BlockSpec((D, T), lambda j: (0, 0)), col, col, col],
        out_specs=[full, col, col],
        out_shape=[jax.ShapeDtypeStruct((T, D), BF), jax.ShapeDtypeStruct((D, D), F32), jax.ShapeDtypeStruct((D, D), F32)],
        scratch_shapes=[pltpu.VMEM((T, D), F32), pltpu.VMEM((T, D), BF), pltpu.VMEM((T, 256), F32)],
        compiler_params=pltpu.CompilerParams(vmem_limit_bytes=56 << 20),
        cost_estimate=pl.CostEstimate(flops=8_000_000_000, bytes_accessed=26_000_000, transcendentals=0),
    )(dq, dk, dv, r1, r2, r3, xt, wq, wk, wv)


def solution(mesh):
    sp_size = mesh.shape['sp']

    def swap(a, bit):
        return lax.ppermute(a, 'sp', [(i, i ^ bit) for i in range(sp_size)])

    def device_step(x, w_q, w_k, w_v, w_o, dy):
        xp, xt, dyp, q, k, v, do, sel = project(x, dy, w_q, w_k, w_v, w_o)
        sel8 = sel[:, 192:288]
        h1, h2, h3 = swap(sel, 1), swap(sel8, 2), swap(sel8, 3)
        at, dq, dk, dv, r1, r2, r3 = attention(q, k, v, do, h1, h2, h3)
        r1, r2, r3 = swap(r1, 1), swap(r2, 2), swap(r3, 3)
        y, dw_o, dw_q = out_stage(at, dyp, w_o, xt, dq)
        dx, dw_k, dw_v = in_stage(dq, dk, dv, r1, r2, r3, xt, w_q, w_k, w_v)
        dw_q, dw_k, dw_v, dw_o = lax.psum((dw_q, dw_k, dw_v, dw_o), 'sp')
        return y, dx, dw_q, dw_k, dw_v, dw_o

    row_spec = P(('dp', 'sp'), None)
    full_spec = P(None, None)
    grad_spec = P('dp', None)
    return jax.shard_map(device_step, mesh=mesh, in_specs=(row_spec, full_spec, full_spec, full_spec, full_spec, row_spec), out_specs=(row_spec, row_spec, grad_spec, grad_spec, grad_spec, grad_spec), check_vma=False)
```

time: 1170 us -> 462 us (0.39); the launches traced: 1150 us -> 462 us
  local copies, waits for them, and re-layouts: 591 us -> 18.3 us
  matrix products: 158 us -> 0 us
  other arithmetic: 89.6 us -> 0 us
  Pallas kernels: 0 us -> 85.9 us
  waiting for transfers between devices: 287 us -> 339 us
    mul x39 -> x0, local copies, waits for them, and re-layouts: 177 us -> none  [the longest x38 175 us: place_rows(): spread = picked[:, None] * eye_f[None, :, None, :, None]]
    dot_general x36 -> x0, matrix products: 158 us -> none  [the longest x4 24.6 us: branch_forward(): jnp.einsum('sacij,sjacd->siacd', attn_probs, v_blk, preferred_element_typ...]
    unnamed x406 -> x22, local copies, waits for them, and re-layouts: 124 us -> 17.3 us
    pallas_call x0 -> x4, Pallas kernels: none -> 85.9 us  [the longest x1 41.1 us: attention(): pl.pallas_call(attention_kernel, grid=(heads,), name='attention', in_spec...]
    reshape x15 -> x0, local copies, waits for them, and re-layouts: 84.7 us -> none  [the longest x12 75.7 us: pick_rows(): values.reshape(n_rows // dilation, dilation, groups, dilation, HEAD_DIM)]
    slice x22 -> x1, local copies, waits for them, and re-layouts: 64.3 us -> 1.02 us  [device_step(): sel8 = sel[:, 192:288]]
    another operation x20 -> x0, local copies, waits for them, and re-layouts: 58.4 us -> none
    mul x5 -> x0, other arithmetic: 41.5 us -> none  [place_rows(): spread = picked[:, None] * eye_f[None, :, None, :, None]]
  transfers between devices with their start and end apart: 17 -> 7, of which waited for: 1 -> 5; matrix products, arithmetic and copies ran while one was open for 52% -> 0% of each run, Pallas kernels for 0% -> 3%
where the time goes in v1:
time: 462 us
  waiting for transfers between devices  339 us (73%)
  Pallas kernels  85.9 us (19%)
  local copies, waits for them, and re-layouts  18.3 us (4%)
  between operations  14.1 us (3%)
  starting transfers between devices  5.22 us (1%)
    psum x1, waiting for transfers between devices, device_step(): dw_q, dw_k, dw_v, dw_o = lax.psum((dw_q, dw_k, dw_v, dw_o), 'sp')  300 us
    pallas_call x1, Pallas kernels, attention(): pl.pallas_call(attention_kernel, grid=(heads,), name='attention', in_spec...  41.1 us
    ppermute x6, waiting for transfers between devices, swap(): return lax.ppermute(a, 'sp', [(i, i ^ bit) for i in range(sp_size)])  38.9 us
    pallas_call x1, Pallas kernels, in_stage(): pl.pallas_call(in_kernel, grid=(4,), name='in_stage', in_specs=[tcol, tco...  17.4 us
    unnamed x22, local copies, waits for them, and re-layouts  17.3 us
    pallas_call x1, Pallas kernels, project(): pl.pallas_call(project_kernel, grid=(4,), name='project', in_specs=[full,...  13.7 us
    pallas_call x1, Pallas kernels, out_stage(): pl.pallas_call(out_kernel, grid=(4,), name='out_stage', in_specs=[full, t...  13.7 us
  transfers between devices with their start and end apart: 7, of which 5 were waited for; matrix products, arithmetic and copies ran while one was open for 0% of the time, Pallas kernels for 3%

profile of v1, /device:TPU:0, one launch (start us, length us, event | category | flops | bytes accessed | tf_op | source)
XLA Modules:
  0.0 462.1 jit_solution(17127236422085625642)
XLA Ops:
  7.2 0.0 all-reduce.3.cloned.1.call-start
  7.2 13.7 %project.1 = (bf16[768,1024]{1,0:T(8,128)(2,1)}, bf16[1024,768]{1,0:T(8,128)(2,1)}, bf16[768,1024]{1,0:T(8,128)(2,1)}, bf16[768,1024]{1,0:T(8,128)(2,1)}, bf16[7...) custom-call(bf16[768,1024]{1,0:T(8,128)(2,1)} %x_ref.1, ...), custom_call_target="tpu_custom_call" | custom-call | flops 6499999744 | bytes 24000000 | tf_op jit(solution)/shard_map/project/pallas_call | solution.py:90
  20.9 0.6 collective-permute-start
  21.5 1.0 slice.3
  22.5 2.7 collective-permute-start.2
  25.2 0.0 collective-permute-start.1
  25.2 9.5 %collective-permute-done.2.h3_ref = bf16[2,96,1024]{2,1,0:T(8,128)(2,1)S(1)} collective-permute-done((bf16[2,96,1024]{2,1,0:T(8,128)(2,1)S(1)}, bf16[2,96,1024]{2,1,0:T(8,128)(2,1)S(1)}, u32[]{:S(2)}, u32[]{:S(2)}) %collective-permute-start.2) | collective-permute-done | bytes 393248 | tf_op jit(solution)/shard_map/ppermute | solution.py:319
  34.7 0.0 copy-start.7
  34.7 8.6 %collective-permute-done.1.h2_ref = bf16[2,96,1024]{2,1,0:T(8,128)(2,1)S(1)} collective-permute-done((bf16[2,96,1024]{2,1,0:T(8,128)(2,1)S(1)}, bf16[2,96,1024]{2,1,0:T(8,128)(2,1)S(1)}, u32[]{:S(2)}, u32[]{:S(2)}) %collective-permute-start.1) | collective-permute-done | bytes 393248 | tf_op jit(solution)/shard_map/ppermute | solution.py:319
  43.3 0.0 copy-start.8
  43.3 0.0 collective-permute-done.h1_ref
  43.3 0.0 copy-start.4
  43.3 0.0 copy-done.7
  43.4 0.7 copy-done.8
  44.1 0.5 copy-done.4
  44.5 41.1 %attention.1 = (bf16[8,2,48,1024]{3,2,1,0:T(8,128)(2,1)}, bf16[8,2,48,1024]{3,2,1,0:T(8,128)(2,1)}, f32[8,2,48,1024]{3,2,1,0:T(8,128)}, f32[8,2,48,1024]{3,2,1,0...) custom-call(bf16[8,2,48,1024]{3,2,1,0:T(8,128)(2,1)} %bitcast.12, ...), custom_call_target="tpu_custom_call" | custom-call | flops 30000001024 | bytes 24000000 | tf_op jit(solution)/shard_map/attention/pallas_call | solution.py:227
  85.7 0.1 collective-permute-start.3
  85.7 1.7 collective-permute-start.4
  87.5 0.1 collective-permute-start.5
  87.6 13.7 %out_stage.1 = (bf16[768,1024]{1,0:T(8,128)(2,1)}, f32[1024,1024]{1,0:T(8,128)}, f32[1024,1024]{1,0:T(8,128)}) custom-call(bf16[768,1024]{1,0:T(8,128)(2,1)} %bitcast.16, bf16[768,1024]{1,0:T(8,128)(2,1)} %bitcast.17, bf16[768,1024]{1,0:T(8,128)(2,1)} %get-tuple-element.32.dyp_ref, bf16[1024,1024]{1,0:T(8,128)(2,1)} %wo_ref.3, ...), custom_call_target="tpu_custom_call" | custom-call | flops 5000000000 | bytes 20000000 | tf_op jit(solution)/shard_map/out_stage/pallas_call | solution.py:254
  101.2 5.0 %collective-permute-done.4.r2_ref = f32[2,96,1024]{2,1,0:T(8,128)S(1)} collective-permute-done((f32[2,96,1024]{2,1,0:T(8,128)}, f32[2,96,1024]{2,1,0:T(8,128)S(1)}, u32[]{:S(2)}, u32[]{:S(2)}) %collective-permute-start.4) | collective-permute-done | bytes 786464 | tf_op jit(solution)/shard_map/ppermute | solution.py:319
  106.2 0.0 copy-start.5
  106.2 15.8 %collective-permute-done.5.r3_ref = f32[2,96,1024]{2,1,0:T(8,128)S(1)} collective-permute-done((f32[2,96,1024]{2,1,0:T(8,128)}, f32[2,96,1024]{2,1,0:T(8,128)S(1)}, u32[]{:S(2)}, u32[]{:S(2)}) %collective-permute-start.5) | collective-permute-done | bytes 786464 | tf_op jit(solution)/shard_map/ppermute | solution.py:319
  122.0 0.0 copy-start.6
  122.0 0.0 collective-permute-done.3.r1_ref
  122.0 0.0 copy-start.3
  122.0 0.0 copy-done.5
  122.0 0.9 copy-done.6
  122.9 0.8 copy-done.3
  123.7 17.4 %in_stage.1 = (bf16[768,1024]{1,0:T(8,128)(2,1)}, f32[1024,1024]{1,0:T(8,128)}, f32[1024,1024]{1,0:T(8,128)}) custom-call(bf16[768,1024]{1,0:T(8,128)(2,1)} %bitcast.11, f32[768,1024]{1,0:T(8,128)} %bitcast.8, f32[768,1024]{1,0:T(8,128)} %bitcast.9, f32[2,288,1024]{2,1,0:T(8,128)} %copy-done.3, f32[2,96,1024]{2,1,0:T(8,128)} %copy-done.5, ...), custom_call_target="tpu_custom_call" | custom-call | flops 8000000000 | bytes 26000000 | tf_op jit(solution)/shard_map/in_stage/pallas_call | solution.py:304
  141.1 0.0 all-reduce.3.cloned.1.call-update
  141.2 299.7 %all-reduce.3.cloned.1.call-done = (f32[1024,1024]{1,0:T(8,128)}, f32[1024,1024]{1,0:T(8,128)}, f32[1024,1024]{1,0:T(8,128)}, f32[1024,1024]{1,0:T(8,128)}) async-done(((f32[1024,1024]{1,0:T(8,128)}, f32[1024,1024]{1,0:T(8,128)}, f32[1024,1024]{1,0:T(8,128)}, f32[1024,1024]{1,0:T(8,128)}), (f32[1024,1024]{1,0:T(8,128)}, f32[1024,1024]{1,0:T(8,128)}, f32[1024,1024]{1,0:T(8,128)}, ...) | async-done | bytes 16777232 | tf_op jit(solution)/shard_map/psum | solution.py:329
  440.9 0.0 copy-start.2
  440.9 4.9 %copy.16 = f32[1024,1024]{1,0:T(8,128)} copy(f32[1024,1024]{1,0:T(8,128)} %get-tuple-element.52) | data formatting | bytes 8388608
  445.8 0.0 copy-done.2
  445.8 0.0 copy-start.1
  445.8 2.1 copy.17
  447.9 1.6 copy-done.1
  449.5 0.0 copy-start
  449.5 2.1 copy.18
  451.6 1.6 copy-done
  453.2 2.0 copy.19
Async XLA Ops:
  7.2 433.7 %all-reduce.3.cloned.1.call-start = ((), (), s32[]{:S(2)}) async-start(), calls=%async_computation | async-start | bytes 33554432 | tf_op jit(solution)/shard_map/psum | solution.py:329
  20.9 22.4 %collective-permute-start = (bf16[2,288,1024]{2,1,0:T(8,128)(2,1)}, bf16[2,288,1024]{2,1,0:T(8,128)(2,1)S(1)}, u32[]{:S(2)}, u32[]{:S(2)}) collective-permute-start(bf16[2,288,1024]{2,1,0:T(8,128)(2,1)} %get-tuple-element.30), channel_id=1, source_target_pairs={{0,1},{1,0},{2,3},{3,2},{4,5},{5,4},{6,7},{7,6},{8,9},{9,8},{10,11... | collective-permute-start | bytes 3538952 | tf_op jit(solution)/shard_map/ppermute | solution.py:319
  22.5 12.2 %collective-permute-start.2 = (bf16[2,96,1024]{2,1,0:T(8,128)(2,1)S(1)}, bf16[2,96,1024]{2,1,0:T(8,128)(2,1)S(1)}, u32[]{:S(2)}, u32[]{:S(2)}) collective-permute-start(bf16[2,96,1024]{2,1,0:T(8,128)(2,1)S(1)} %slice.3), channel_id=1, source_target_pairs={{0,3},{1,2},{2,1},{3,0},{4,7},{5,6},{6,5},{7,4},{8,11},{9,10},{10,... | collective-permute-start | bytes 1179656 | tf_op jit(solution)/shard_map/ppermute | solution.py:319
  25.2 18.1 %collective-permute-start.1 = (bf16[2,96,1024]{2,1,0:T(8,128)(2,1)S(1)}, bf16[2,96,1024]{2,1,0:T(8,128)(2,1)S(1)}, u32[]{:S(2)}, u32[]{:S(2)}) collective-permute-start(bf16[2,96,1024]{2,1,0:T(8,128)(2,1)S(1)} %slice.3), channel_id=1, source_target_pairs={{0,2},{1,3},{2,0},{3,1},{4,6},{5,7},{6,4},{7,5},{8,10},{9,11},{10,... | collective-permute-start | bytes 1179656 | tf_op jit(solution)/shard_map/ppermute | solution.py:319
  34.7 8.6 %copy-start.7 = (bf16[2,96,1024]{2,1,0:T(8,128)(2,1)}, bf16[2,96,1024]{2,1,0:T(8,128)(2,1)S(1)}, u32[]{:S(2)}) copy-start(bf16[2,96,1024]{2,1,0:T(8,128)(2,1)S(1)} %collective-permute-done.2.h3_ref) | copy-start | bytes 1179652
  43.3 0.7 copy-start.8
  43.3 1.2 copy-start.4
  85.7 36.3 %collective-permute-start.3 = (f32[2,288,1024]{2,1,0:T(8,128)}, f32[2,288,1024]{2,1,0:T(8,128)S(1)}, u32[]{:S(2)}, u32[]{:S(2)}) collective-permute-start(f32[2,288,1024]{2,1,0:T(8,128)} %get-tuple-element.38), channel_id=1, source_target_pairs={{0,1},{1,0},{2,3},{3,2},{4,5},{5,4},{6,7},{7,6},{8,9},{9,8},{10,11... | collective-permute-start | bytes 7077896 | tf_op jit(solution)/shard_map/ppermute | solution.py:319
  85.7 20.5 %collective-permute-start.4 = (f32[2,96,1024]{2,1,0:T(8,128)}, f32[2,96,1024]{2,1,0:T(8,128)S(1)}, u32[]{:S(2)}, u32[]{:S(2)}) collective-permute-start(f32[2,96,1024]{2,1,0:T(8,128)} %get-tuple-element.39), channel_id=1, source_target_pairs={{0,2},{1,3},{2,0},{3,1},{4,6},{5,7},{6,4},{7,5},{8,10},{9,11},{10,... | collective-permute-start | bytes 2359304 | tf_op jit(solution)/shard_map/ppermute | solution.py:319
  87.5 34.5 %collective-permute-start.5 = (f32[2,96,1024]{2,1,0:T(8,128)}, f32[2,96,1024]{2,1,0:T(8,128)S(1)}, u32[]{:S(2)}, u32[]{:S(2)}) collective-permute-start(f32[2,96,1024]{2,1,0:T(8,128)} %get-tuple-element.40), channel_id=1, source_target_pairs={{0,3},{1,2},{2,1},{3,0},{4,7},{5,6},{6,5},{7,4},{8,11},{9,10},{10,... | collective-permute-start | bytes 2359304 | tf_op jit(solution)/shard_map/ppermute | solution.py:319
  106.2 15.8 %copy-start.5 = (f32[2,96,1024]{2,1,0:T(8,128)}, f32[2,96,1024]{2,1,0:T(8,128)S(1)}, u32[]{:S(2)}) copy-start(f32[2,96,1024]{2,1,0:T(8,128)S(1)} %collective-permute-done.4.r2_ref) | copy-start | bytes 2359300
  122.0 0.9 copy-start.6
  122.0 1.7 copy-start.3
  440.9 4.9 %copy-start.2 = (f32[1024,1024]{1,0:T(8,128)S(1)}, f32[1024,1024]{1,0:T(8,128)}, u32[]{:S(2)}) copy-start(f32[1024,1024]{1,0:T(8,128)} %get-tuple-element.53) | copy-start | bytes 12582916
  445.8 3.7 copy-start.1
  449.5 3.7 copy-start
Sparse Core Ops, SparseCore 0:
  141.3 299.5 all-reduce.2

commit v2 on v1

--- a/solution.py
+++ b/solution.py
@@ -240,32 +240,36 @@
     return f(at), f(dq), f(dk), f(dv), r1, r2, r3
 
 
-def out_kernel(at_ref, att_ref, dyp_ref, wo_ref, xt_ref, dq_ref, y_ref, dwo_ref, dwq_ref, yp_ref):
+def out_kernel(at_ref, wo_ref, y_ref, att_ref, yp_ref):
+    j = pl.program_id(0)
     yp_ref[...] = dot(at_ref[...], wo_ref[...]).astype(BF)
     unpermute_into(yp_ref, y_ref)
-    dwo_ref[...] = dot(att_ref[...].T, dyp_ref[...])
-    dwq_ref[...] = dot(xt_ref[...], dq_ref[...])
-
-
-def out_stage(at, dyp, wo, xt, dq):
+
+    @pl.when(j == 0)
+    def _():
+        for i in range(8):
+            att_ref[128 * i:128 * i + 128, :] = at_ref[:, 128 * i:128 * i + 128].T
+
+
+def out_stage(at, wo):
     full = pl.BlockSpec((T, D), lambda j: (0, 0))
     col = pl.BlockSpec((D, 256), lambda j: (0, j))
     tcol = pl.BlockSpec((T, 256), lambda j: (0, j))
     return pl.pallas_call(
         out_kernel, grid=(4,), name='out_stage',
-        in_specs=[full, tcol, full, col, pl.BlockSpec((D, T), lambda j: (0, 0)), tcol],
-        out_specs=[tcol, pl.BlockSpec((256, D), lambda j: (j, 0)), col],
-        out_shape=[jax.ShapeDtypeStruct((T, D), BF), jax.ShapeDtypeStruct((D, D), F32), jax.ShapeDtypeStruct((D, D), F32)],
+        in_specs=[full, col],
+        out_specs=[tcol, pl.BlockSpec((D, T), lambda j: (0, 0))],
+        out_shape=[jax.ShapeDtypeStruct((T, D), BF), jax.ShapeDtypeStruct((D, T), BF)],
         scratch_shapes=[pltpu.VMEM((T, 256), BF)],
         compiler_params=pltpu.CompilerParams(vmem_limit_bytes=56 << 20),
-        cost_estimate=pl.CostEstimate(flops=5_000_000_000, bytes_accessed=20_000_000, transcendentals=0),
-    )(at, at, dyp, wo, xt, dq)
-
-
-def in_kernel(dq_ref, dk_ref, dv_ref, r1_ref, r2_ref, r3_ref, xt_ref, wq_ref, wk_ref, wv_ref, dx_ref, dwk_ref, dwv_ref, acc_ref, dxp_ref, sum_ref):
+        cost_estimate=pl.CostEstimate(flops=1_700_000_000, bytes_accessed=8_000_000, transcendentals=0),
+    )(at, wo)
+
+
+def in_kernel(dq_ref, dk_ref, dv_ref, r1_ref, r2_ref, r3_ref, wq_ref, wk_ref, wv_ref, dx_ref, dkb_ref, dvb_ref, acc_ref, dxp_ref, sum_ref):
     j = pl.program_id(0)
     part = dot_nt(dq_ref[...], wq_ref[...])
-    for which, (own_ref, w_ref, dw_ref) in enumerate(((dk_ref, wk_ref, dwk_ref), (dv_ref, wv_ref, dwv_ref))):
+    for which, (own_ref, w_ref, g_ref) in enumerate(((dk_ref, wk_ref, dkb_ref), (dv_ref, wv_ref, dvb_ref))):
         sum_ref[...] = own_ref[...]
         for i in range(2):
             s4, s8 = starts(2 * j + i)
@@ -277,9 +281,8 @@
                 zero = jnp.zeros_like(add)
                 sum_ref[pl.ds(pl.multiple_of(first * CH, CH), n), cols] += jnp.where(keep, add, zero)
                 sum_ref[pl.ds(pl.multiple_of(first * CH + NK, CH), n), cols] += jnp.where(keep, zero, add)
-        g = sum_ref[...].astype(BF)
-        dw_ref[...] = dot(xt_ref[...], g)
-        part = part + dot_nt(g, w_ref[...])
+        g_ref[...] = sum_ref[...].astype(BF)
+        part = part + dot_nt(g_ref[...], w_ref[...])
 
     @pl.when(j == 0)
     def _():
@@ -295,7 +298,7 @@
         unpermute_into(dxp_ref, dx_ref)
 
 
-def in_stage(dq, dk, dv, r1, r2, r3, xt, wq, wk, wv):
+def in_stage(dq, dk, dv, r1, r2, r3, wq, wk, wv):
     full = pl.BlockSpec((T, D), lambda j: (0, 0))
     col = pl.BlockSpec((D, 256), lambda j: (0, j))
     tcol = pl.BlockSpec((T, 256), lambda j: (0, j))
@@ -303,13 +306,143 @@
     small = pl.BlockSpec((2, 96, 256), lambda j: (0, 0, j))
     return pl.pallas_call(
         in_kernel, grid=(4,), name='in_stage',
-        in_specs=[tcol, tcol, tcol, big, small, small, pl.BlockSpec((D, T), lambda j: (0, 0)), col, col, col],
-        out_specs=[full, col, col],
-        out_shape=[jax.ShapeDtypeStruct((T, D), BF), jax.ShapeDtypeStruct((D, D), F32), jax.ShapeDtypeStruct((D, D), F32)],
+        in_specs=[tcol, tcol, tcol, big, small, small, col, col, col],
+        out_specs=[full, tcol, tcol],
+        out_shape=[jax.ShapeDtypeStruct((T, D), BF)] * 3,
         scratch_shapes=[pltpu.VMEM((T, D), F32), pltpu.VMEM((T, D), BF), pltpu.VMEM((T, 256), F32)],
         compiler_params=pltpu.CompilerParams(vmem_limit_bytes=56 << 20),
-        cost_estimate=pl.CostEstimate(flops=8_000_000_000, bytes_accessed=26_000_000, transcendentals=0),
-    )(dq, dk, dv, r1, r2, r3, xt, wq, wk, wv)
+        cost_estimate=pl.CostEstimate(flops=5_000_000_000, bytes_accessed=16_000_000, transcendentals=0),
+    )(dq, dk, dv, r1, r2, r3, wq, wk, wv)
+
+
+STEPS = 8
+PAIRS = tuple((d, u) for u in range(2) for d in range(2))
+
+
+def ring_kernel(xt_ref, att_ref, dq_ref, dk_ref, dv_ref, dy_ref, *refs):
+    (outs, (acc, prt, stage, rs_send, rs_recv, pt_send, pt_recv, ag_send, ag_recv, cc_send, cc_recv, lo_sem)) = (refs[:4], refs[4:])
+    out = ((outs[0], outs[1]), (outs[2], outs[3]))
+    lhs = ((att_ref, xt_ref), (xt_ref, xt_ref))
+    rhs = ((dy_ref, dq_ref), (dk_ref, dv_ref))
+    s = lax.axis_index('sp')
+    core, y, z = s % 2, (s // 2) % 2, s // 4
+    pos = z + y * (7 - 2 * z)
+    mate = {'sp': s + 1 - 2 * core}
+
+    def member(r):
+        r = r % STEPS
+        row = r // 4
+        return {'sp': (r + row * (7 - 2 * r)) * 4 + row * 2 + core}
+
+    ahead = (member(pos + 1), member(pos + STEPS - 1))
+    mine = pl.ds(pl.multiple_of(512 * core, 512), 512)
+    other = pl.ds(pl.multiple_of(512 * (1 - core), 512), 512)
+
+    def shard(d, step):
+        return (pos + 15 - step) % STEPS if d == 0 else (pos + 1 + step) % STEPS
+
+    def rows(i):
+        return pl.ds(pl.multiple_of(128 * i, 128), 128)
+
+    def partial(d, u, step, cols):
+        return dot(lhs[d][u][rows(shard(d, step)), :], rhs[d][u][:, cols])
+
+    def remote(src, dst, send, recv, peer):
+        return pltpu.make_async_remote_copy(src_ref=src, dst_ref=dst, send_sem=send, recv_sem=recv, device_id=peer, device_id_type=pl.DeviceIdType.MESH)
+
+    def to_mate(d, u, step):
+        return remote(stage.at[d, u, step % 2], prt.at[d, u, step], pt_send.at[d, u, step], pt_recv.at[d, u, step], mate)
+
+    def to_next(d, u, step):
+        return remote(acc.at[d, u, step], acc.at[d, u, step + 1], rs_send.at[d, u, step], rs_recv.at[d, u, step], ahead[d])
+
+    def give(d, u, step):
+        stage[d, u, step % 2] = partial(d, u, step, other)
+        to_mate(d, u, step).start()
+
+    def spread(d, u, t):
+        i = (pos + 8 - t) % STEPS if d == 0 else (pos + t) % STEPS
+        return out[d][u].at[rows(i), mine]
+
+    def gather_next(d, u, t, src):
+        return remote(src, spread(d, u, t), ag_send.at[d, u, t], ag_recv.at[d, u, t], ahead[d])
+
+    def gather_mate(d, u, t, src):
+        return remote(src, spread(d, u, t), cc_send.at[d, u, t], cc_recv.at[d, u, t], mate)
+
+    for d, u in PAIRS:
+        give(d, u, 0)
+    for d, u in PAIRS:
+        acc[d, u, 0] = partial(d, u, 0, mine)
+        to_mate(d, u, 0).wait_recv()
+        acc[d, u, 0] += prt[d, u, 0]
+        to_next(d, u, 0).start()
+    for d, u in PAIRS:
+        give(d, u, 1)
+
+    def reduce_step(step, carry):
+        for d, u in PAIRS:
+            part = partial(d, u, step, mine)
+            to_mate(d, u, step).wait_recv()
+            to_next(d, u, step - 1).wait_recv()
+            acc[d, u, step] += prt[d, u, step] + part
+            to_next(d, u, step).start()
+        for d, u in PAIRS:
+            to_mate(d, u, step - 1).wait_send()
+            give(d, u, step + 1)
+        return carry
+
+    lax.fori_loop(1, STEPS - 1, reduce_step, 0)
+    last = STEPS - 1
+    for d, u in PAIRS:
+        part = partial(d, u, last, mine)
+        to_mate(d, u, last).wait_recv()
+        to_next(d, u, last - 1).wait_recv()
+        acc[d, u, last] += prt[d, u, last] + part
+        src = acc.at[d, u, last]
+        gather_next(d, u, 0, src).start()
+        gather_mate(d, u, 0, src).start()
+        pltpu.make_async_copy(src, spread(d, u, 0), lo_sem.at[d, u]).start()
+
+    def gather_step(t, carry):
+        for d, u in PAIRS:
+            gather_next(d, u, t - 1, acc.at[d, u, last]).wait_recv()
+            gather_next(d, u, t, spread(d, u, t)).start()
+            gather_mate(d, u, t, spread(d, u, t)).start()
+        return carry
+
+    lax.fori_loop(1, STEPS - 1, gather_step, 0)
+    for d, u in PAIRS:
+        gather_next(d, u, last - 1, acc.at[d, u, last]).wait_recv()
+        gather_mate(d, u, last, spread(d, u, last)).start()
+
+    def drain(t, carry):
+        for d, u in PAIRS:
+            to_next(d, u, t).wait_send()
+            gather_next(d, u, t, acc.at[d, u, last]).wait_send()
+            gather_mate(d, u, t, acc.at[d, u, last]).wait()
+        return carry
+
+    lax.fori_loop(0, last, drain, 0)
+    for d, u in PAIRS:
+        gather_mate(d, u, last, acc.at[d, u, last]).wait()
+        to_mate(d, u, last - 1).wait_send()
+        to_mate(d, u, last).wait_send()
+        pltpu.make_async_copy(acc.at[d, u, last], spread(d, u, 0), lo_sem.at[d, u]).wait()
+
+
+def ring_stage(xt, att, dq, dk, dv, dyp):
+    sem = lambda n: pltpu.SemaphoreType.DMA((2, 2, n))
+    return pl.pallas_call(
+        ring_kernel, name='ring_stage',
+        in_specs=[pl.BlockSpec(memory_space=pltpu.VMEM)] * 6,
+        out_specs=[pl.BlockSpec(memory_space=pl.ANY)] * 4,
+        out_shape=[jax.ShapeDtypeStruct((D, D), F32)] * 4,
+        scratch_shapes=[pltpu.VMEM((2, 2, STEPS, 128, 512), F32), pltpu.VMEM((2, 2, STEPS, 128, 512), F32), pltpu.VMEM((2, 2, 2, 128, 512), F32),
+                        sem(7), sem(7), sem(8), sem(8), sem(7), sem(7), sem(8), sem(8), pltpu.SemaphoreType.DMA((2, 2))],
+        compiler_params=pltpu.CompilerParams(has_side_effects=True, vmem_limit_bytes=56 << 20),
+        cost_estimate=pl.CostEstimate(flops=7_000_000_000, bytes_accessed=40_000_000, transcendentals=0),
+    )(xt, att, dq, dk, dv, dyp)
 
 
 def solution(mesh):
@@ -324,9 +457,9 @@
         h1, h2, h3 = swap(sel, 1), swap(sel8, 2), swap(sel8, 3)
         at, dq, dk, dv, r1, r2, r3 = attention(q, k, v, do, h1, h2, h3)
         r1, r2, r3 = swap(r1, 1), swap(r2, 2), swap(r3, 3)
-        y, dw_o, dw_q = out_stage(at, dyp, w_o, xt, dq)
-        dx, dw_k, dw_v = in_stage(dq, dk, dv, r1, r2, r3, xt, w_q, w_k, w_v)
-        dw_q, dw_k, dw_v, dw_o = lax.psum((dw_q, dw_k, dw_v, dw_o), 'sp')
+        y, att = out_stage(at, w_o)
+        dx, dkb, dvb = in_stage(dq, dk, dv, r1, r2, r3, w_q, w_k, w_v)
+        dw_o, dw_q, dw_k, dw_v = ring_stage(xt, att, dq, dkb, dvb, dyp)
         return y, dx, dw_q, dw_k, dw_v, dw_o
 
     row_spec = P(('dp', 'sp'), None)

time: 462 us -> 320 us (0.69)
  waiting for transfers between devices: 339 us -> 45 us
  Pallas kernels: 85.9 us -> 250 us
  between operations: 14.1 us -> 0.68 us
    psum x1 -> x0, waiting for transfers between devices: 300 us -> none  [device_step(): dw_q, dw_k, dw_v, dw_o = lax.psum((dw_q, dw_k, dw_v, dw_o), 'sp')]
    pallas_call x1 -> x2, Pallas kernels: 13.7 us -> 183 us  [the longest x1 175 us: ring_stage(): pl.pallas_call(ring_kernel, name='ring_stage', in_specs=[pl.BlockSpec(mem...]
    ppermute x6, waiting for transfers between devices: 38.9 us -> 45 us  [swap(): return lax.ppermute(a, 'sp', [(i, i ^ bit) for i in range(sp_size)])]
    pallas_call x1, Pallas kernels: 17.4 us -> 12.6 us  [in_stage(): pl.pallas_call(in_kernel, grid=(4,), name='in_stage', in_specs=[tcol, tco...]
  transfers between devices with their start and end apart: 7 -> 6, of which waited for: 5 -> 4; matrix products, arithmetic and copies ran while one was open for 0% -> 0% of each run, Pallas kernels for 3% -> 2%
where the time goes in v2:
time: 320 us; the launch traced here: 319 us
  Pallas kernels  250 us (78%)
  waiting for transfers between devices  45 us (14%)
  local copies, waits for them, and re-layouts  18.2 us (6%)
  starting transfers between devices  5.19 us (2%)
    pallas_call x1, Pallas kernels, ring_stage(): pl.pallas_call(ring_kernel, name='ring_stage', in_specs=[pl.BlockSpec(mem...  175 us
    ppermute x6, waiting for transfers between devices, swap(): return lax.ppermute(a, 'sp', [(i, i ^ bit) for i in range(sp_size)])  45 us
    pallas_call x1, Pallas kernels, attention(): pl.pallas_call(attention_kernel, grid=(heads,), name='attention', in_spec...  41.2 us
    unnamed x22, local copies, waits for them, and re-layouts  17.2 us
    pallas_call x1, Pallas kernels, project(): pl.pallas_call(project_kernel, grid=(4,), name='project', in_specs=[full,...  13.7 us
    pallas_call x1, Pallas kernels, in_stage(): pl.pallas_call(in_kernel, grid=(4,), name='in_stage', in_specs=[tcol, tco...  12.6 us
    pallas_call x1, Pallas kernels, out_stage(): pl.pallas_call(out_kernel, grid=(4,), name='out_stage', in_specs=[full, c...  7.49 us
  transfers between devices with their start and end apart: 6, of which 4 were waited for; matrix products, arithmetic and copies ran while one was open for 0% of the time, Pallas kernels for 2%

profile of v2, /device:TPU:0, one launch (start us, length us, event | category | flops | bytes accessed | tf_op | source)
XLA Modules:
  0.0 319.2 jit_solution(17299283890912155085)
XLA Ops:
  0.6 13.7 %project.1 = (bf16[768,1024]{1,0:T(8,128)(2,1)}, bf16[1024,768]{1,0:T(8,128)(2,1)}, bf16[768,1024]{1,0:T(8,128)(2,1)}, bf16[768,1024]{1,0:T(8,128)(2,1)}, bf16[7...) custom-call(bf16[768,1024]{1,0:T(8,128)(2,1)} %x_ref.1, ...), custom_call_target="tpu_custom_call" | custom-call | flops 6499999744 | bytes 24000000 | tf_op jit(solution)/shard_map/project/pallas_call | solution.py:90
  14.4 0.6 collective-permute-start
  14.9 1.0 slice.3
  16.0 2.7 collective-permute-start.2
  18.7 0.0 collective-permute-start.1
  18.7 9.5 %collective-permute-done.2.h3_ref = bf16[2,96,1024]{2,1,0:T(8,128)(2,1)S(1)} collective-permute-done((bf16[2,96,1024]{2,1,0:T(8,128)(2,1)S(1)}, bf16[2,96,1024]{2,1,0:T(8,128)(2,1)S(1)}, u32[]{:S(2)}, u32[]{:S(2)}) %collective-permute-start.2) | collective-permute-done | bytes 393248 | tf_op jit(solution)/shard_map/ppermute | solution.py:452
  28.1 0.0 copy-start.7
  28.1 8.6 %collective-permute-done.1.h2_ref = bf16[2,96,1024]{2,1,0:T(8,128)(2,1)S(1)} collective-permute-done((bf16[2,96,1024]{2,1,0:T(8,128)(2,1)S(1)}, bf16[2,96,1024]{2,1,0:T(8,128)(2,1)S(1)}, u32[]{:S(2)}, u32[]{:S(2)}) %collective-permute-start.1) | collective-permute-done | bytes 393248 | tf_op jit(solution)/shard_map/ppermute | solution.py:452
  36.8 0.0 copy-start.8
  36.8 0.0 collective-permute-done.h1_ref
  36.8 0.0 copy-start.4
  36.8 0.0 copy-done.7
  36.8 0.7 copy-done.8
  37.5 0.4 copy-done.4
  37.9 41.2 %attention.1 = (bf16[8,2,48,1024]{3,2,1,0:T(8,128)(2,1)}, bf16[8,2,48,1024]{3,2,1,0:T(8,128)(2,1)}, f32[8,2,48,1024]{3,2,1,0:T(8,128)}, f32[8,2,48,1024]{3,2,1,0...) custom-call(bf16[8,2,48,1024]{3,2,1,0:T(8,128)(2,1)} %bitcast.12, ...), custom_call_target="tpu_custom_call" | custom-call | flops 30000001024 | bytes 24000000 | tf_op jit(solution)/shard_map/attention/pallas_call | solution.py:227
  79.1 0.1 collective-permute-start.3
  79.2 1.7 collective-permute-start.4
  80.9 0.1 collective-permute-start.5
  81.0 7.5 %out_stage.1 = (bf16[768,1024]{1,0:T(8,128)(2,1)}, bf16[1024,768]{1,0:T(8,128)(2,1)}) custom-call(bf16[768,1024]{1,0:T(8,128)(2,1)} %bitcast.16, bf16[1024,1024]{1,0:T(8,128)(2,1)} %wo_ref.3), custom_call_target="tpu_custom_call" | custom-call | flops 1700000000 | bytes 8000000 | tf_op jit(solution)/shard_map/out_stage/pallas_call | solution.py:258
  88.5 11.1 %collective-permute-done.4.r2_ref = f32[2,96,1024]{2,1,0:T(8,128)S(1)} collective-permute-done((f32[2,96,1024]{2,1,0:T(8,128)}, f32[2,96,1024]{2,1,0:T(8,128)S(1)}, u32[]{:S(2)}, u32[]{:S(2)}) %collective-permute-start.4) | collective-permute-done | bytes 786464 | tf_op jit(solution)/shard_map/ppermute | solution.py:452
  99.6 0.0 copy-start.5
  99.7 15.8 %collective-permute-done.5.r3_ref = f32[2,96,1024]{2,1,0:T(8,128)S(1)} collective-permute-done((f32[2,96,1024]{2,1,0:T(8,128)}, f32[2,96,1024]{2,1,0:T(8,128)S(1)}, u32[]{:S(2)}, u32[]{:S(2)}) %collective-permute-start.5) | collective-permute-done | bytes 786464 | tf_op jit(solution)/shard_map/ppermute | solution.py:452
  115.4 0.0 copy-start.6
  115.4 0.0 collective-permute-done.3.r1_ref
  115.4 0.0 copy-start.3
  115.4 0.0 copy-done.5
  115.4 0.9 copy-done.6
  116.3 0.8 copy-done.3
  117.1 12.6 %in_stage.1 = (bf16[768,1024]{1,0:T(8,128)(2,1)}, bf16[768,1024]{1,0:T(8,128)(2,1)}, bf16[768,1024]{1,0:T(8,128)(2,1)}) custom-call(bf16[768,1024]{1,0:T(8,128)(2,1)} %bitcast.10, f32[768,1024]{1,0:T(8,128)} %bitcast.8, f32[768,1024]{1,0:T(8,128)} %bitcast.9, f32[2,288,1024]{2,1,0:T(8,128)} %copy-done.3, f32[2,96,1024]{2,1,0:T(8,128)} %copy-done.5, ...), custom_call_target="tpu_custom_call" | custom-call | flops 5000000000 | bytes 16000000 | tf_op jit(solution)/shard_map/in_stage/pallas_call | solution.py:307
  129.7 175.1 %ring_stage.1 = (f32[1024,1024]{1,0:T(8,128)}, f32[1024,1024]{1,0:T(8,128)}, f32[1024,1024]{1,0:T(8,128)}, f32[1024,1024]{1,0:T(8,128)}) custom-call(bf16[1024,768]{1,0:T(8,128)(2,1)} %get-tuple-element.43.xt_ref, bf16[1024,768]{1,0:T(8,128)(2,1)} %get-tuple-element.44.att_ref, bf16[768,1024]{1,0:T(8,128)(2,1)} %bitcast.11, ...), custom_call_target="tpu_custom_call" | custom-call | flops 7000000000 | bytes 40000000 | tf_op jit(solution)/shard_map/ring_stage/pallas_call | solution.py:436
  304.8 0.0 copy-start.2
  304.8 4.9 %copy.16 = f32[1024,1024]{1,0:T(8,128)} copy(f32[1024,1024]{1,0:T(8,128)} %get-tuple-element.60) | data formatting | bytes 8388608
  309.7 0.0 copy-done.2
  309.7 0.0 copy-start.1
  309.7 2.1 copy.17
  311.9 1.6 copy-done.1
  313.4 0.0 copy-start
  313.4 2.1 copy.18
  315.6 1.6 copy-done
  317.1 2.0 copy.19
Async XLA Ops:
  14.4 22.4 %collective-permute-start = (bf16[2,288,1024]{2,1,0:T(8,128)(2,1)}, bf16[2,288,1024]{2,1,0:T(8,128)(2,1)S(1)}, u32[]{:S(2)}, u32[]{:S(2)}) collective-permute-start(bf16[2,288,1024]{2,1,0:T(8,128)(2,1)} %get-tuple-element.33), channel_id=1, source_target_pairs={{0,1},{1,0},{2,3},{3,2},{4,5},{5,4},{6,7},{7,6},{8,9},{9,8},{10,11... | collective-permute-start | bytes 3538952 | tf_op jit(solution)/shard_map/ppermute | solution.py:452
  16.0 12.2 %collective-permute-start.2 = (bf16[2,96,1024]{2,1,0:T(8,128)(2,1)S(1)}, bf16[2,96,1024]{2,1,0:T(8,128)(2,1)S(1)}, u32[]{:S(2)}, u32[]{:S(2)}) collective-permute-start(bf16[2,96,1024]{2,1,0:T(8,128)(2,1)S(1)} %slice.3), channel_id=1, source_target_pairs={{0,3},{1,2},{2,1},{3,0},{4,7},{5,6},{6,5},{7,4},{8,11},{9,10},{10,... | collective-permute-start | bytes 1179656 | tf_op jit(solution)/shard_map/ppermute | solution.py:452
  18.7 18.1 %collective-permute-start.1 = (bf16[2,96,1024]{2,1,0:T(8,128)(2,1)S(1)}, bf16[2,96,1024]{2,1,0:T(8,128)(2,1)S(1)}, u32[]{:S(2)}, u32[]{:S(2)}) collective-permute-start(bf16[2,96,1024]{2,1,0:T(8,128)(2,1)S(1)} %slice.3), channel_id=1, source_target_pairs={{0,2},{1,3},{2,0},{3,1},{4,6},{5,7},{6,4},{7,5},{8,10},{9,11},{10,... | collective-permute-start | bytes 1179656 | tf_op jit(solution)/shard_map/ppermute | solution.py:452
  28.1 8.6 %copy-start.7 = (bf16[2,96,1024]{2,1,0:T(8,128)(2,1)}, bf16[2,96,1024]{2,1,0:T(8,128)(2,1)S(1)}, u32[]{:S(2)}) copy-start(bf16[2,96,1024]{2,1,0:T(8,128)(2,1)S(1)} %collective-permute-done.2.h3_ref) | copy-start | bytes 1179652
  36.8 0.7 copy-start.8
  36.8 1.2 copy-start.4
  79.1 36.3 %collective-permute-start.3 = (f32[2,288,1024]{2,1,0:T(8,128)}, f32[2,288,1024]{2,1,0:T(8,128)S(1)}, u32[]{:S(2)}, u32[]{:S(2)}) collective-permute-start(f32[2,288,1024]{2,1,0:T(8,128)} %get-tuple-element.39), channel_id=1, source_target_pairs={{0,1},{1,0},{2,3},{3,2},{4,5},{5,4},{6,7},{7,6},{8,9},{9,8},{10,11... | collective-permute-start | bytes 7077896 | tf_op jit(solution)/shard_map/ppermute | solution.py:452
  79.2 20.5 %collective-permute-start.4 = (f32[2,96,1024]{2,1,0:T(8,128)}, f32[2,96,1024]{2,1,0:T(8,128)S(1)}, u32[]{:S(2)}, u32[]{:S(2)}) collective-permute-start(f32[2,96,1024]{2,1,0:T(8,128)} %get-tuple-element.40), channel_id=1, source_target_pairs={{0,2},{1,3},{2,0},{3,1},{4,6},{5,7},{6,4},{7,5},{8,10},{9,11},{10,... | collective-permute-start | bytes 2359304 | tf_op jit(solution)/shard_map/ppermute | solution.py:452
  80.9 34.5 %collective-permute-start.5 = (f32[2,96,1024]{2,1,0:T(8,128)}, f32[2,96,1024]{2,1,0:T(8,128)S(1)}, u32[]{:S(2)}, u32[]{:S(2)}) collective-permute-start(f32[2,96,1024]{2,1,0:T(8,128)} %get-tuple-element.41), channel_id=1, source_target_pairs={{0,3},{1,2},{2,1},{3,0},{4,7},{5,6},{6,5},{7,4},{8,11},{9,10},{10,... | collective-permute-start | bytes 2359304 | tf_op jit(solution)/shard_map/ppermute | solution.py:452
  99.6 15.8 %copy-start.5 = (f32[2,96,1024]{2,1,0:T(8,128)}, f32[2,96,1024]{2,1,0:T(8,128)S(1)}, u32[]{:S(2)}) copy-start(f32[2,96,1024]{2,1,0:T(8,128)S(1)} %collective-permute-done.4.r2_ref) | copy-start | bytes 2359300
  115.4 0.9 copy-start.6
  115.4 1.7 copy-start.3
  304.8 5.0 %copy-start.2 = (f32[1024,1024]{1,0:T(8,128)S(1)}, f32[1024,1024]{1,0:T(8,128)}, u32[]{:S(2)}) copy-start(f32[1024,1024]{1,0:T(8,128)} %get-tuple-element.61) | copy-start | bytes 12582916
  309.7 3.7 %copy-start.1 = (f32[1024,1024]{1,0:T(8,128)S(1)}, f32[1024,1024]{1,0:T(8,128)}, u32[]{:S(2)}) copy-start(f32[1024,1024]{1,0:T(8,128)} %get-tuple-element.62) | copy-start | bytes 12582916
  313.4 3.7 %copy-start = (f32[1024,1024]{1,0:T(8,128)S(1)}, f32[1024,1024]{1,0:T(8,128)}, u32[]{:S(2)}) copy-start(f32[1024,1024]{1,0:T(8,128)} %get-tuple-element.63) | copy-start | bytes 12582916

commit v3 on v2

--- a/solution.py
+++ b/solution.py
@@ -240,10 +240,19 @@
     return f(at), f(dq), f(dk), f(dv), r1, r2, r3
 
 
-def out_kernel(at_ref, wo_ref, y_ref, att_ref, yp_ref):
+def out_kernel(at_ref, wo_ref, dq_ref, wq_ref, y_ref, att_ref, dxq_ref, yp_ref):
     j = pl.program_id(0)
     yp_ref[...] = dot(at_ref[...], wo_ref[...]).astype(BF)
     unpermute_into(yp_ref, y_ref)
+    part = dot_nt(dq_ref[...], wq_ref[...])
+
+    @pl.when(j == 0)
+    def _():
+        dxq_ref[...] = part
+
+    @pl.when(j > 0)
+    def _():
+        dxq_ref[...] += part
 
     @pl.when(j == 0)
     def _():
@@ -251,42 +260,43 @@
             att_ref[128 * i:128 * i + 128, :] = at_ref[:, 128 * i:128 * i + 128].T
 
 
-def out_stage(at, wo):
+def out_stage(at, wo, dq, wq):
     full = pl.BlockSpec((T, D), lambda j: (0, 0))
     col = pl.BlockSpec((D, 256), lambda j: (0, j))
     tcol = pl.BlockSpec((T, 256), lambda j: (0, j))
     return pl.pallas_call(
         out_kernel, grid=(4,), name='out_stage',
-        in_specs=[full, col],
-        out_specs=[tcol, pl.BlockSpec((D, T), lambda j: (0, 0))],
-        out_shape=[jax.ShapeDtypeStruct((T, D), BF), jax.ShapeDtypeStruct((D, T), BF)],
+        in_specs=[full, col, tcol, col],
+        out_specs=[tcol, pl.BlockSpec((D, T), lambda j: (0, 0)), full],
+        out_shape=[jax.ShapeDtypeStruct((T, D), BF), jax.ShapeDtypeStruct((D, T), BF), jax.ShapeDtypeStruct((T, D), F32)],
         scratch_shapes=[pltpu.VMEM((T, 256), BF)],
         compiler_params=pltpu.CompilerParams(vmem_limit_bytes=56 << 20),
-        cost_estimate=pl.CostEstimate(flops=1_700_000_000, bytes_accessed=8_000_000, transcendentals=0),
-    )(at, wo)
-
-
-def in_kernel(dq_ref, dk_ref, dv_ref, r1_ref, r2_ref, r3_ref, wq_ref, wk_ref, wv_ref, dx_ref, dkb_ref, dvb_ref, acc_ref, dxp_ref, sum_ref):
+        cost_estimate=pl.CostEstimate(flops=3_300_000_000, bytes_accessed=15_000_000, transcendentals=0),
+    )(at, wo, dq, wq)
+
+
+def in_kernel(dxq_ref, dk_ref, dv_ref, r1_ref, r2_ref, wk_ref, wv_ref, dx_ref, dkb_ref, dvb_ref, acc_ref, dxp_ref, sum_ref):
     j = pl.program_id(0)
-    part = dot_nt(dq_ref[...], wq_ref[...])
+    part = None
     for which, (own_ref, w_ref, g_ref) in enumerate(((dk_ref, wk_ref, dkb_ref), (dv_ref, wv_ref, dvb_ref))):
         sum_ref[...] = own_ref[...]
         for i in range(2):
             s4, s8 = starts(2 * j + i)
             cols = slice(128 * i, 128 * i + 128)
             a4 = r1_ref[which, 0:192, cols]
-            a8 = r1_ref[which, 192:288, cols] + r2_ref[which, :, cols] + r3_ref[which, :, cols]
+            a8 = r1_ref[which, 192:288, cols] + r2_ref[which, :, cols]
             for first, n, add in ((s4, 192, a4), (s8, 96, a8)):
                 keep = left_lanes(n)
                 zero = jnp.zeros_like(add)
                 sum_ref[pl.ds(pl.multiple_of(first * CH, CH), n), cols] += jnp.where(keep, add, zero)
                 sum_ref[pl.ds(pl.multiple_of(first * CH + NK, CH), n), cols] += jnp.where(keep, zero, add)
         g_ref[...] = sum_ref[...].astype(BF)
-        part = part + dot_nt(g_ref[...], w_ref[...])
+        term = dot_nt(g_ref[...], w_ref[...])
+        part = term if part is None else part + term
 
     @pl.when(j == 0)
     def _():
-        acc_ref[...] = part
+        acc_ref[...] = dxq_ref[...] + part
 
     @pl.when(j > 0)
     def _():
@@ -298,7 +308,7 @@
         unpermute_into(dxp_ref, dx_ref)
 
 
-def in_stage(dq, dk, dv, r1, r2, r3, wq, wk, wv):
+def in_stage(dxq, dk, dv, r1, r2, wk, wv):
     full = pl.BlockSpec((T, D), lambda j: (0, 0))
     col = pl.BlockSpec((D, 256), lambda j: (0, j))
     tcol = pl.BlockSpec((T, 256), lambda j: (0, j))
@@ -306,13 +316,13 @@
     small = pl.BlockSpec((2, 96, 256), lambda j: (0, 0, j))
     return pl.pallas_call(
         in_kernel, grid=(4,), name='in_stage',
-        in_specs=[tcol, tcol, tcol, big, small, small, col, col, col],
+        in_specs=[full, tcol, tcol, big, small, col, col],
         out_specs=[full, tcol, tcol],
         out_shape=[jax.ShapeDtypeStruct((T, D), BF)] * 3,
         scratch_shapes=[pltpu.VMEM((T, D), F32), pltpu.VMEM((T, D), BF), pltpu.VMEM((T, 256), F32)],
         compiler_params=pltpu.CompilerParams(vmem_limit_bytes=56 << 20),
         cost_estimate=pl.CostEstimate(flops=5_000_000_000, bytes_accessed=16_000_000, transcendentals=0),
-    )(dq, dk, dv, r1, r2, r3, wq, wk, wv)
+    )(dxq, dk, dv, r1, r2, wk, wv)
 
 
 STEPS = 8
@@ -454,11 +464,13 @@
     def device_step(x, w_q, w_k, w_v, w_o, dy):
         xp, xt, dyp, q, k, v, do, sel = project(x, dy, w_q, w_k, w_v, w_o)
         sel8 = sel[:, 192:288]
-        h1, h2, h3 = swap(sel, 1), swap(sel8, 2), swap(sel8, 3)
+        h2 = swap(sel8, 2)
+        h1, h3 = swap(sel, 1), swap(h2, 1)
         at, dq, dk, dv, r1, r2, r3 = attention(q, k, v, do, h1, h2, h3)
-        r1, r2, r3 = swap(r1, 1), swap(r2, 2), swap(r3, 3)
-        y, att = out_stage(at, w_o)
-        dx, dkb, dvb = in_stage(dq, dk, dv, r1, r2, r3, w_q, w_k, w_v)
+        r2 = swap(r2 + swap(r3, 1), 2)
+        r1 = swap(r1, 1)
+        y, att, dxq = out_stage(at, w_o, dq, w_q)
+        dx, dkb, dvb = in_stage(dxq, dk, dv, r1, r2, w_k, w_v)
         dw_o, dw_q, dw_k, dw_v = ring_stage(xt, att, dq, dkb, dvb, dyp)
         return y, dx, dw_q, dw_k, dw_v, dw_o
 

time: 320 us -> 303 us (0.947)
  waiting for transfers between devices: 45 us -> 20.5 us
  Pallas kernels: 250 us -> 257 us
    ppermute x6, waiting for transfers between devices: 45 us -> 20.5 us  [swap(): return lax.ppermute(a, 'sp', [(i, i ^ bit) for i in range(sp_size)])]
    pallas_call x1, Pallas kernels: 7.49 us -> 14 us  [out_stage(): pl.pallas_call(out_kernel, grid=(4,), name='out_stage', in_specs=[full, c...]
    unnamed x22 -> x20, local copies, waits for them, and re-layouts: 17.2 us -> 17.2 us
  transfers between devices with their start and end apart: 6 -> 6, of which waited for: 4 -> 4; matrix products, arithmetic and copies ran while one was open for 0% -> 1% of each run, Pallas kernels for 2% -> 5%
where the time goes in v3:
time: 303 us
  Pallas kernels  257 us (85%)
  waiting for transfers between devices  20.5 us (7%)
  local copies, waits for them, and re-layouts  18.2 us (6%)
  starting transfers between devices  5.54 us (2%)
    pallas_call x1, Pallas kernels, ring_stage(): pl.pallas_call(ring_kernel, name='ring_stage', in_specs=[pl.BlockSpec(mem...  175 us
    pallas_call x1, Pallas kernels, attention(): pl.pallas_call(attention_kernel, grid=(heads,), name='attention', in_spec...  41.1 us
    ppermute x6, waiting for transfers between devices, swap(): return lax.ppermute(a, 'sp', [(i, i ^ bit) for i in range(sp_size)])  20.5 us
    unnamed x20, local copies, waits for them, and re-layouts  17.2 us
    pallas_call x1, Pallas kernels, out_stage(): pl.pallas_call(out_kernel, grid=(4,), name='out_stage', in_specs=[full, c...  14 us
    pallas_call x1, Pallas kernels, project(): pl.pallas_call(project_kernel, grid=(4,), name='project', in_specs=[full,...  13.7 us
    pallas_call x1, Pallas kernels, in_stage(): pl.pallas_call(in_kernel, grid=(4,), name='in_stage', in_specs=[full, tco...  12.7 us
  transfers between devices with their start and end apart: 6, of which 4 were waited for; matrix products, arithmetic and copies ran while one was open for 1% of the time, Pallas kernels for 5%

profile of v3, /device:TPU:0, one launch (start us, length us, event | category | flops | bytes accessed | tf_op | source)
XLA Modules:
  0.0 302.9 jit_solution(16316355888425091548)
XLA Ops:
  0.6 13.7 %project.1 = (bf16[768,1024]{1,0:T(8,128)(2,1)}, bf16[1024,768]{1,0:T(8,128)(2,1)}, bf16[768,1024]{1,0:T(8,128)(2,1)}, bf16[768,1024]{1,0:T(8,128)(2,1)}, bf16[7...) custom-call(bf16[768,1024]{1,0:T(8,128)(2,1)} %x_ref.1, ...), custom_call_target="tpu_custom_call" | custom-call | flops 6499999744 | bytes 24000000 | tf_op jit(solution)/shard_map/project/pallas_call | solution.py:90
  14.4 0.6 collective-permute-start
  14.9 1.0 slice.3
  16.0 2.6 collective-permute-start.1
  18.6 9.8 %collective-permute-done.1.h2_ref = bf16[2,96,1024]{2,1,0:T(8,128)(2,1)S(1)} collective-permute-done((bf16[2,96,1024]{2,1,0:T(8,128)(2,1)S(1)}, bf16[2,96,1024]{2,1,0:T(8,128)(2,1)S(1)}, u32[]{:S(2)}, u32[]{:S(2)}) %collective-permute-start.1) | collective-permute-done | bytes 393248 | tf_op jit(solution)/shard_map/ppermute | solution.py:462
  28.3 0.0 copy-start.6
  28.3 0.0 collective-permute-start.2
  28.3 1.7 collective-permute-done.2.h3_ref
  30.1 0.0 copy-start.7
  30.1 0.0 collective-permute-done.h1_ref
  30.1 0.0 copy-start.4
  30.1 0.0 copy-done.6
  30.1 0.8 copy-done.7
  30.8 0.4 copy-done.4
  31.2 41.1 %attention.1 = (bf16[8,2,48,1024]{3,2,1,0:T(8,128)(2,1)}, bf16[8,2,48,1024]{3,2,1,0:T(8,128)(2,1)}, f32[8,2,48,1024]{3,2,1,0:T(8,128)}, f32[8,2,48,1024]{3,2,1,0...) custom-call(bf16[8,2,48,1024]{3,2,1,0:T(8,128)(2,1)} %bitcast.12, ...), custom_call_target="tpu_custom_call" | custom-call | flops 30000001024 | bytes 24000000 | tf_op jit(solution)/shard_map/attention/pallas_call | solution.py:227
  72.4 0.2 collective-permute-start.3
  72.6 0.4 collective-permute-start.4
  72.9 5.1 %collective-permute-done.4 = f32[2,96,1024]{2,1,0:T(8,128)S(1)} collective-permute-done((f32[2,96,1024]{2,1,0:T(8,128)}, f32[2,96,1024]{2,1,0:T(8,128)S(1)}, u32[]{:S(2)}, u32[]{:S(2)}) %collective-permute-start.4) | collective-permute-done | bytes 786464 | tf_op jit(solution)/shard_map/ppermute | solution.py:462
  78.1 1.2 add.3
  79.3 1.8 collective-permute-start.5
  81.1 14.0 %out_stage.1 = (bf16[768,1024]{1,0:T(8,128)(2,1)}, bf16[1024,768]{1,0:T(8,128)(2,1)}, f32[768,1024]{1,0:T(8,128)}) custom-call(bf16[768,1024]{1,0:T(8,128)(2,1)} %bitcast.16, bf16[1024,1024]{1,0:T(8,128)(2,1)} %wo_ref.3, bf16[768,1024]{1,0:T(8,128)(2,1)} %bitcast.10, bf16[1024,1024]{1,0:T(8,128)(2,1)} %wq_ref.3), custom_call_target="tpu_custom_call" | custom-call | flops 3300000000 | bytes 15000000 | tf_op jit(solution)/shard_map/out_stage/pallas_call | solution.py:267
  95.1 3.9 %collective-permute-done.5.r2_ref = f32[2,96,1024]{2,1,0:T(8,128)S(1)} collective-permute-done((f32[2,96,1024]{2,1,0:T(8,128)S(1)}, f32[2,96,1024]{2,1,0:T(8,128)S(1)}, u32[]{:S(2)}, u32[]{:S(2)}) %collective-permute-start.5) | collective-permute-done | bytes 786464 | tf_op jit(solution)/shard_map/ppermute | solution.py:462
  99.0 0.0 copy-start.5
  99.0 0.0 collective-permute-done.3.r1_ref
  99.0 0.0 copy-start.3
  99.0 0.9 copy-done.5
  99.9 0.8 copy-done.3
  100.7 12.7 %in_stage.1 = (bf16[768,1024]{1,0:T(8,128)(2,1)}, bf16[768,1024]{1,0:T(8,128)(2,1)}, bf16[768,1024]{1,0:T(8,128)(2,1)}) custom-call(f32[768,1024]{1,0:T(8,128)} %get-tuple-element.38.dxq_ref, f32[768,1024]{1,0:T(8,128)} %bitcast.8, f32[768,1024]{1,0:T(8,128)} %bitcast.9, f32[2,288,1024]{2,1,0:T(8,128)} %copy-done.3, f32[2,96,1024]{2,1,0:T(8,128)} %copy-done.5, ...), custom_call_target="tpu_custom_call" | custom-call | flops 5000000000 | bytes 16000000 | tf_op jit(solution)/shard_map/in_stage/pallas_call | solution.py:317
  113.3 175.2 %ring_stage.1 = (f32[1024,1024]{1,0:T(8,128)}, f32[1024,1024]{1,0:T(8,128)}, f32[1024,1024]{1,0:T(8,128)}, f32[1024,1024]{1,0:T(8,128)}) custom-call(bf16[1024,768]{1,0:T(8,128)(2,1)} %get-tuple-element.45.xt_ref, bf16[1024,768]{1,0:T(8,128)(2,1)} %get-tuple-element.46.att_ref, bf16[768,1024]{1,0:T(8,128)(2,1)} %bitcast.11, ...), custom_call_target="tpu_custom_call" | custom-call | flops 7000000000 | bytes 40000000 | tf_op jit(solution)/shard_map/ring_stage/pallas_call | solution.py:446
  288.5 0.0 copy-start.2
  288.5 4.9 %copy.16 = f32[1024,1024]{1,0:T(8,128)} copy(f32[1024,1024]{1,0:T(8,128)} %get-tuple-element.62) | data formatting | bytes 8388608
  293.4 0.0 copy-done.2
  293.5 0.0 copy-start.1
  293.5 2.1 copy.17
  295.6 1.6 copy-done.1
  297.2 0.0 copy-start
  297.2 2.1 copy.18
  299.3 1.6 copy-done
  300.9 2.0 copy.19
Async XLA Ops:
  14.4 15.7 %collective-permute-start = (bf16[2,288,1024]{2,1,0:T(8,128)(2,1)}, bf16[2,288,1024]{2,1,0:T(8,128)(2,1)S(1)}, u32[]{:S(2)}, u32[]{:S(2)}) collective-permute-start(bf16[2,288,1024]{2,1,0:T(8,128)(2,1)} %get-tuple-element.34), channel_id=1, source_target_pairs={{0,1},{1,0},{2,3},{3,2},{4,5},{5,4},{6,7},{7,6},{8,9},{9,8},{10,11... | collective-permute-start | bytes 3538952 | tf_op jit(solution)/shard_map/ppermute | solution.py:462
  16.0 12.4 %collective-permute-start.1 = (bf16[2,96,1024]{2,1,0:T(8,128)(2,1)S(1)}, bf16[2,96,1024]{2,1,0:T(8,128)(2,1)S(1)}, u32[]{:S(2)}, u32[]{:S(2)}) collective-permute-start(bf16[2,96,1024]{2,1,0:T(8,128)(2,1)S(1)} %slice.3), channel_id=1, source_target_pairs={{0,2},{1,3},{2,0},{3,1},{4,6},{5,7},{6,4},{7,5},{8,10},{9,11},{10,... | collective-permute-start | bytes 1179656 | tf_op jit(solution)/shard_map/ppermute | solution.py:462
  28.3 1.7 copy-start.6
  28.3 1.7 collective-permute-start.2
  30.1 0.8 copy-start.7
  30.1 1.2 copy-start.4
  72.4 26.6 %collective-permute-start.3 = (f32[2,288,1024]{2,1,0:T(8,128)}, f32[2,288,1024]{2,1,0:T(8,128)S(1)}, u32[]{:S(2)}, u32[]{:S(2)}) collective-permute-start(f32[2,288,1024]{2,1,0:T(8,128)} %get-tuple-element.41), channel_id=1, source_target_pairs={{0,1},{1,0},{2,3},{3,2},{4,5},{5,4},{6,7},{7,6},{8,9},{9,8},{10,11... | collective-permute-start | bytes 7077896 | tf_op jit(solution)/shard_map/ppermute | solution.py:462
  72.6 5.5 %collective-permute-start.4 = (f32[2,96,1024]{2,1,0:T(8,128)}, f32[2,96,1024]{2,1,0:T(8,128)S(1)}, u32[]{:S(2)}, u32[]{:S(2)}) collective-permute-start(f32[2,96,1024]{2,1,0:T(8,128)} %get-tuple-element.43), channel_id=1, source_target_pairs={{0,1},{1,0},{2,3},{3,2},{4,5},{5,4},{6,7},{7,6},{8,9},{9,8},{10,11... | collective-permute-start | bytes 2359304 | tf_op jit(solution)/shard_map/ppermute | solution.py:462
  79.3 19.7 %collective-permute-start.5 = (f32[2,96,1024]{2,1,0:T(8,128)S(1)}, f32[2,96,1024]{2,1,0:T(8,128)S(1)}, u32[]{:S(2)}, u32[]{:S(2)}) collective-permute-start(f32[2,96,1024]{2,1,0:T(8,128)S(1)} %add.3), channel_id=1, source_target_pairs={{0,2},{1,3},{2,0},{3,1},{4,6},{5,7},{6,4},{7,5},{8,10},{9,11},{10,... | collective-permute-start | bytes 2359304 | tf_op jit(solution)/shard_map/ppermute | solution.py:462
  99.0 0.9 copy-start.5
  99.0 1.7 copy-start.3
  288.5 5.0 %copy-start.2 = (f32[1024,1024]{1,0:T(8,128)S(1)}, f32[1024,1024]{1,0:T(8,128)}, u32[]{:S(2)}) copy-start(f32[1024,1024]{1,0:T(8,128)} %get-tuple-element.63) | copy-start | bytes 12582916
  293.5 3.7 %copy-start.1 = (f32[1024,1024]{1,0:T(8,128)S(1)}, f32[1024,1024]{1,0:T(8,128)}, u32[]{:S(2)}) copy-start(f32[1024,1024]{1,0:T(8,128)} %get-tuple-element.64) | copy-start | bytes 12582916
  297.2 3.7 %copy-start = (f32[1024,1024]{1,0:T(8,128)S(1)}, f32[1024,1024]{1,0:T(8,128)}, u32[]{:S(2)}) copy-start(f32[1024,1024]{1,0:T(8,128)} %get-tuple-element.65) | copy-start | bytes 12582916

commit v4 on v2

v4 whole, which is shorter than its diff:
```python
import jax
import jax.numpy as jnp
from jax import lax
from jax.experimental import pallas as pl
from jax.experimental.pallas import tpu as pltpu
from jax.sharding import PartitionSpec as P


BF = jnp.bfloat16
F32 = jnp.float32
T = 768
D = 1024
CH = 96
NK = 384
LANE = 128
TILE = 256
HALF = 512
SEG = 48
ROWS = 192
HALO = 288
HEAD = 64
MIB = 1 << 20
NT = (((1,), (1,)), ((), ()))


def cost(work):
    return pl.CostEstimate(flops=work * 10**8, bytes_accessed=work * 10**6, transcendentals=0)


def dot(a, b):
    return jnp.dot(a, b, preferred_element_type=F32)


def dot_nt(a, b):
    return lax.dot_general(a, b, NT, preferred_element_type=F32)


def perm_matrix(inverse):
    a = lax.broadcasted_iota(jnp.int32, (LANE, LANE), 1 if inverse else 0)
    b = lax.broadcasted_iota(jnp.int32, (LANE, LANE), 0 if inverse else 1)
    c = a // 16
    res = 4 * (c % 2) + 2 * ((c // 2) % 2) + c // 4
    src = (a % 16) * 8 + res
    return jnp.where(src == b, 1.0, 0.0).astype(BF)


def permute_into(src_ref, dst_ref):
    m = perm_matrix(False)
    for blk in range(T // LANE):
        z = dot(m, src_ref[blk * LANE:(blk + 1) * LANE, :]).astype(BF)
        for c in range(8):
            dst_ref[c * CH + blk * 16:c * CH + blk * 16 + 16, :] = z[c * 16:c * 16 + 16, :]


def unpermute_into(src_ref, dst_ref):
    m = perm_matrix(True)
    for blk in range(T // LANE):
        z = jnp.concatenate([src_ref[c * CH + blk * 16:c * CH + blk * 16 + 16, :] for c in range(8)], axis=0)
        dst_ref[blk * LANE:(blk + 1) * LANE, :] = dot(m, z).astype(BF)


def starts(p):
    return 2 * (p % 2), 2 * (p % 2) + (p // 2) % 2


def left_lanes(n):
    return lax.broadcasted_iota(jnp.int32, (n, LANE), 1) < HEAD


def keys_kernel(x_ref, wk_ref, wv_ref, xp_ref, k_ref, v_ref, sel_ref):
    j = pl.program_id(0)

    @pl.when(j == 0)
    def _():
        permute_into(x_ref, xp_ref)

    k_ref[...] = dot(xp_ref[...], wk_ref[...]).astype(BF)
    v_ref[...] = dot(xp_ref[...], wv_ref[...]).astype(BF)
    for i in range(2):
        s4, s8 = starts(2 * j + i)
        cols = slice(LANE * i, LANE * i + LANE)
        for which, src in enumerate((k_ref, v_ref)):
            for first, n, at in ((s4, ROWS, 0), (s8, CH, ROWS)):
                even = src[pl.ds(pl.multiple_of(first * CH, CH), n), cols]
                odd = src[pl.ds(pl.multiple_of(first * CH + NK, CH), n), cols]
                sel_ref[which, at:at + n, cols] = jnp.where(left_lanes(n), even, odd)


def queries_kernel(xp_ref, dy_ref, wq_ref, wo_ref, xt_ref, dyp_ref, q_ref, do_ref):
    j = pl.program_id(0)

    @pl.when(j == 0)
    def _():
        permute_into(dy_ref, dyp_ref)

    for i in range(2):
        lanes = pl.ds(pl.multiple_of(TILE * j + LANE * i, LANE), LANE)
        xt_ref[LANE * i:LANE * i + LANE, :] = xp_ref[:, lanes].T
    q_ref[...] = (dot(xp_ref[...], wq_ref[...]).astype(BF) * 0.125).astype(BF)
    do_ref[...] = dot_nt(dyp_ref[...], wo_ref[...]).astype(BF)


def project(x, dy, wq, wk, wv, wo):
    full = pl.BlockSpec((T, D), lambda j: (0, 0))
    wcol = pl.BlockSpec((D, TILE), lambda j: (0, j))
    wrow = pl.BlockSpec((TILE, D), lambda j: (j, 0))
    tcol = pl.BlockSpec((T, TILE), lambda j: (0, j))
    tok = jax.ShapeDtypeStruct((T, D), BF)
    price = cost(33)
    xp, k, v, sel = pl.pallas_call(
        keys_kernel, grid=(4,), name='project_keys',
        in_specs=[full, wcol, wcol],
        out_specs=[full, tcol, tcol, pl.BlockSpec((2, HALO, TILE), lambda j: (0, 0, j))],
        out_shape=[tok, tok, tok, jax.ShapeDtypeStruct((2, HALO, D), BF)],
        compiler_params=pltpu.CompilerParams(vmem_limit_bytes=63 * MIB), cost_estimate=price,
    )(x, wk, wv)
    xt, dyp, q, do = pl.pallas_call(
        queries_kernel, grid=(4,), name='project_queries',
        in_specs=[full, full, wcol, wrow],
        out_specs=[pl.BlockSpec((TILE, T), lambda j: (j, 0)), full, tcol, tcol],
        out_shape=[jax.ShapeDtypeStruct((D, T), BF), tok, tok, tok],
        compiler_params=pltpu.CompilerParams(vmem_limit_bytes=63 * MIB), cost_estimate=price,
    )(xp, dy, wq, wo)
    return xt, dyp, q, k, v, do, sel


def attention_kernel(q_ref, k_ref, v_ref, do_ref, h1_ref, h2_ref, h3_ref,
                     at_ref, dq_ref, dk_ref, dv_ref, r1_ref, r2_ref, r3_ref,
                     e_ref, m_ref, acc_ref, dqa_ref, de_ref):
    p = pl.program_id(0)
    s4, s8 = starts(p)
    left = left_lanes(NK)

    def rows_of(ref, first, n):
        return ref[pl.ds(first, n // CH)].reshape(n, ref.shape[-1])

    def pick(ref, b):
        if b < 2:
            return ref[:, b].reshape(NK, LANE)
        first, n = BLOCKS[b]
        return jnp.where(left[:n], rows_of(ref, first, n), rows_of(ref, first + 4, n))

    BLOCKS = {0: (None, NK), 1: (None, NK), 2: (0, NK), 3: (s4, ROWS), 4: (s8, CH)}
    OFFS = (0, NK, T, 1152, 1344)

    def keys(ref, which, b):
        own = pick(ref, b)
        if b < 3:
            return own
        if b == 3:
            return jnp.concatenate([own, h1_ref[which, 0:ROWS, :]], axis=0)
        return jnp.concatenate([own, h1_ref[which, ROWS:HALO, :], h2_ref[which], h3_ref[which]], axis=0)

    def get(ref, e, b):
        w = ref.shape[-1]
        if b < 2:
            return ref[e, :, b].reshape(NK, w)
        first, n = BLOCKS[b]
        return ref[e, pl.ds(first + 4 * e, n // CH)].reshape(n, w)

    def put(ref, e, b, val):
        w = ref.shape[-1]
        if b < 2:
            ref[e, :, b] = val.reshape(8, SEG, w)
        else:
            first, n = BLOCKS[b]
            ref[e, pl.ds(first + 4 * e, n // CH)] = val.reshape(n // CH, 2, SEG, w)

    def head(val, e):
        keep = left[:val.shape[0]] if e == 0 else jnp.logical_not(left[:val.shape[0]])
        return jnp.where(keep, val, jnp.zeros_like(val))

    def wide(val):
        return jnp.concatenate([val, val, val], axis=1)

    for b in range(5):
        n = BLOCKS[b][1]
        qs, ks = pick(q_ref, b), keys(k_ref, 0, b)
        for e in range(2):
            s = dot_nt(head(qs, e), ks)
            e_ref[e, OFFS[b]:OFFS[b] + n, :] = s
            mx = jnp.broadcast_to(jnp.max(s, axis=1, keepdims=True), (n, LANE))
            if b >= 2:
                mx = jnp.maximum(mx, get(m_ref, e, b))
            put(m_ref, e, b, mx)
    ones = jnp.ones((NK, LANE), BF)
    for b in range(5):
        n = BLOCKS[b][1]
        vo = jnp.concatenate([keys(v_ref, 1, b), ones], axis=1)
        for e in range(2):
            ex = jnp.exp(e_ref[e, OFFS[b]:OFFS[b] + n, :] - wide(get(m_ref, e, b)))
            e_ref[e, OFFS[b]:OFFS[b] + n, :] = ex
            o = dot(ex.astype(BF), vo)
            if b >= 2:
                o = o + get(acc_ref, e, b)
            put(acc_ref, e, b, o)
    for c in range(8):
        outs = []
        dd = do_ref[c].reshape(CH, LANE).astype(F32)
        for e in range(2):
            acc = acc_ref[e, c].reshape(CH, TILE)
            linv = 1.0 / acc[:, LANE:]
            o = acc[:, :LANE] * linv
            outs.append(o)
            de = jnp.sum(head(dd * o, e), axis=1, keepdims=True)
            m_ref[e, c] = linv.reshape(2, SEG, LANE)
            de_ref[e, c] = jnp.broadcast_to(de, (CH, LANE)).reshape(2, SEG, LANE)
        at_ref[c] = jnp.where(left[:CH], outs[0], outs[1]).astype(BF).reshape(2, SEG, LANE)
    for b in range(5):
        n = BLOCKS[b][1]
        qs, ks, dos, vs = pick(q_ref, b), keys(k_ref, 0, b), pick(do_ref, b), keys(v_ref, 1, b)
        qt, dot_t = qs.T, dos.T
        dkt, dvt = [], []
        for e in range(2):
            half = slice(HEAD * e, HEAD * e + HEAD)
            pn = e_ref[e, OFFS[b]:OFFS[b] + n, :] * wide(get(m_ref, e, b))
            dp = dot_nt(head(dos, e), vs)
            ds = (pn * (dp - wide(get(de_ref, e, b)))).astype(BF)
            dvt.append(dot(dot_t[half], pn.astype(BF)))
            dkt.append(dot(qt[half], ds))
            dq = dot(ds, ks)
            if b >= 2:
                dq = dq + get(dqa_ref, e, b)
            put(dqa_ref, e, b, dq)
        for which, (parts, own_ref) in enumerate(((dkt, dk_ref), (dvt, dv_ref))):
            g = jnp.concatenate(parts, axis=0).T
            if b < 2:
                own_ref[:, b] = g.reshape(8, SEG, LANE)
                continue
            first = BLOCKS[b][0]
            own = g[:n]
            zero = jnp.zeros_like(own)
            c = n // CH
            shape = (c, 2, SEG, LANE)
            own_ref[pl.ds(first, c)] += jnp.where(left[:n], own, zero).reshape(shape)
            own_ref[pl.ds(first + 4, c)] += jnp.where(left[:n], zero, own).reshape(shape)
            if b == 3:
                r1_ref[which, 0:ROWS, :] = g[ROWS:]
            if b == 4:
                r1_ref[which, ROWS:HALO, :] = g[CH:ROWS]
                r2_ref[which] = g[ROWS:HALO]
                r3_ref[which] = g[HALO:NK]
    for c in range(8):
        pair = jnp.where(left[:CH], dqa_ref[0, c].reshape(CH, LANE), dqa_ref[1, c].reshape(CH, LANE)) * 0.125
        dq_ref[c] = pair.astype(BF).reshape(2, SEG, LANE)


def attention(half, earlier, q, k, v, do, h1, h2, h3):
    row = pl.BlockSpec((8, 2, SEG, LANE), lambda p: (0, 0, 0, p + 4 * half))
    big = pl.BlockSpec((2, HALO, LANE), lambda p: (0, 0, p + 4 * half))
    small = pl.BlockSpec((2, CH, LANE), lambda p: (0, 0, p + 4 * half))
    rbig = pl.BlockSpec((2, HALO, LANE), lambda p: (0, 0, p))
    rsmall = pl.BlockSpec((2, CH, LANE), lambda p: (0, 0, p))
    r = lambda a: a.reshape(8, 2, SEG, D)

    def body(*refs):
        attention_kernel(*refs[:7], *refs[7 + len(earlier):])

    return pl.pallas_call(
        body, grid=(4,), name='attention',
        in_specs=[row] * 4 + [big, small, small] + [pl.BlockSpec(memory_space=pl.ANY)] * len(earlier),
        out_specs=[row] * 4 + [rbig, rsmall, rsmall],
        out_shape=[jax.ShapeDtypeStruct((8, 2, SEG, D), BF)] * 2 + [jax.ShapeDtypeStruct((8, 2, SEG, D), F32)] * 2
        + [jax.ShapeDtypeStruct((2, HALO, D // 2), F32)] + [jax.ShapeDtypeStruct((2, CH, D // 2), F32)] * 2,
        scratch_shapes=[pltpu.VMEM((2, 1440, NK), F32), pltpu.VMEM((2, 8, 2, SEG, LANE), F32), pltpu.VMEM((2, 8, 2, SEG, TILE), F32),
                        pltpu.VMEM((2, 8, 2, SEG, LANE), F32), pltpu.VMEM((2, 8, 2, SEG, LANE), F32)],
        input_output_aliases={7 + n: n for n in range(len(earlier))},
        compiler_params=pltpu.CompilerParams(vmem_limit_bytes=63 * MIB),
       cost_estimate=cost(150),
    )(r(q), r(k), r(v), r(do), h1, h2, h3, *earlier)


def out_kernel(at_ref, wo_ref, y_ref, att_ref, yp_ref):
    j = pl.program_id(0)
    yp_ref[...] = dot(at_ref[...], wo_ref[...]).astype(BF)
    unpermute_into(yp_ref, y_ref)

    @pl.when(j == 0)
    def _():
        for i in range(8):
            att_ref[LANE * i:LANE * i + LANE, :] = at_ref[:, LANE * i:LANE * i + LANE].T


def out_stage(at, wo):
    full = pl.BlockSpec((T, D), lambda j: (0, 0))
    col = pl.BlockSpec((D, TILE), lambda j: (0, j))
    tcol = pl.BlockSpec((T, TILE), lambda j: (0, j))
    return pl.pallas_call(
        out_kernel, grid=(4,), name='out_stage',
        in_specs=[full, col],
        out_specs=[tcol, pl.BlockSpec((D, T), lambda j: (0, 0))],
        out_shape=[jax.ShapeDtypeStruct((T, D), BF), jax.ShapeDtypeStruct((D, T), BF)],
        scratch_shapes=[pltpu.VMEM((T, TILE), BF)],
        compiler_params=pltpu.CompilerParams(vmem_limit_bytes=63 * MIB),
       cost_estimate=cost(17),
    )(at, wo)


def in_kernel(dk_ref, dv_ref, r1a_ref, r1b_ref, r2a_ref, r2b_ref, dkb_ref, dvb_ref, sum_ref):
    j = pl.program_id(0)
    for which, (own_ref, g_ref) in enumerate(((dk_ref, dkb_ref), (dv_ref, dvb_ref))):
        sum_ref[...] = own_ref[...]
        for i in range(2):
            s4, s8 = starts(2 * j + i)
            cols = slice(LANE * i, LANE * i + LANE)
            one = jnp.where(j < 2, r1a_ref[which, :, cols], r1b_ref[which, :, cols])
            a4 = one[:ROWS]
            a8 = one[ROWS:] + jnp.where(j < 2, r2a_ref[which, :, cols], r2b_ref[which, :, cols])
            for first, n, add in ((s4, ROWS, a4), (s8, CH, a8)):
                keep = left_lanes(n)
                zero = jnp.zeros_like(add)
                sum_ref[pl.ds(pl.multiple_of(first * CH, CH), n), cols] += jnp.where(keep, add, zero)
                sum_ref[pl.ds(pl.multiple_of(first * CH + NK, CH), n), cols] += jnp.where(keep, zero, add)
        g_ref[...] = sum_ref[...].astype(BF)


def in_stage(dk, dv, r1a, r1b, r2a, r2b):
    tcol = pl.BlockSpec((T, TILE), lambda j: (0, j))
    first = lambda n: pl.BlockSpec((2, n, TILE), lambda j: (0, 0, jnp.minimum(j, 1)))
    second = lambda n: pl.BlockSpec((2, n, TILE), lambda j: (0, 0, jnp.maximum(j - 2, 0)))
    return pl.pallas_call(
        in_kernel, grid=(4,), name='in_stage',
        in_specs=[tcol, tcol, first(HALO), second(HALO), first(CH), second(CH)],
        out_specs=[tcol, tcol],
        out_shape=[jax.ShapeDtypeStruct((T, D), BF)] * 2,
        scratch_shapes=[pltpu.VMEM((T, TILE), F32)],
        compiler_params=pltpu.CompilerParams(vmem_limit_bytes=63 * MIB),
       cost_estimate=cost(1),
    )(dk, dv, r1a, r1b, r2a, r2b)


STEPS = 8
PAIRS = tuple((d, u) for u in range(2) for d in range(2))


def ring_kernel(xt_ref, att_ref, dq_ref, dk_ref, dv_ref, dy_ref, wq_hbm, wk_hbm, wv_hbm, *refs):
    outs, dx_ref = refs[:4], refs[4]
    acc, prt, stage, wq_ref, wk_ref, wv_ref, dxp_ref, rs_send, rs_recv, pt_send, pt_recv, ag_send, ag_recv, cc_send, cc_recv, lo_sem, ld_sem = refs[5:]
    loads = [pltpu.make_async_copy(a, b, ld_sem.at[n]) for n, (a, b) in enumerate(((wq_hbm, wq_ref), (wk_hbm, wk_ref), (wv_hbm, wv_ref)))]
    for load in loads:
        load.start()
    out = ((outs[0], outs[1]), (outs[2], outs[3]))
    lhs = ((att_ref, xt_ref), (xt_ref, xt_ref))
    rhs = ((dy_ref, dq_ref), (dk_ref, dv_ref))
    s = lax.axis_index('sp')
    core, y, z = s % 2, (s // 2) % 2, s // 4
    pos = z + y * (7 - 2 * z)
    mate = {'sp': s + 1 - 2 * core}

    def member(r):
        r = r % STEPS
        row = r // 4
        return {'sp': (r + row * (7 - 2 * r)) * 4 + row * 2 + core}

    ahead = (member(pos + 1), member(pos + STEPS - 1))
    mine = pl.ds(pl.multiple_of(HALF * core, HALF), HALF)
    other = pl.ds(pl.multiple_of(HALF * (1 - core), HALF), HALF)

    def shard(d, step):
        return (pos + 15 - step) % STEPS if d == 0 else (pos + 1 + step) % STEPS

    def rows(i):
        return pl.ds(pl.multiple_of(LANE * i, LANE), LANE)

    def partial(d, u, step, cols):
        return dot(lhs[d][u][rows(shard(d, step)), :], rhs[d][u][:, cols])

    def remote(src, dst, send, recv, peer):
        return pltpu.make_async_remote_copy(src_ref=src, dst_ref=dst, send_sem=send, recv_sem=recv, device_id=peer, device_id_type=pl.DeviceIdType.MESH)

    def to_mate(d, u, step):
        return remote(stage.at[d, u, step % 2], prt.at[d, u, step], pt_send.at[d, u, step], pt_recv.at[d, u, step], mate)

    def to_next(d, u, step):
        return remote(acc.at[d, u, step], acc.at[d, u, step + 1], rs_send.at[d, u, step], rs_recv.at[d, u, step], ahead[d])

    def give(d, u, step):
        stage[d, u, step % 2] = partial(d, u, step, other)
        to_mate(d, u, step).start()

    def spread(d, u, t):
        i = (pos + 8 - t) % STEPS if d == 0 else (pos + t) % STEPS
        return out[d][u].at[rows(i), mine]

    def gather_next(d, u, t, src):
        return remote(src, spread(d, u, t), ag_send.at[d, u, t], ag_recv.at[d, u, t], ahead[d])

    def gather_mate(d, u, t, src):
        return remote(src, spread(d, u, t), cc_send.at[d, u, t], cc_recv.at[d, u, t], mate)

    for d, u in PAIRS:
        give(d, u, 0)
    for d, u in PAIRS:
        acc[d, u, 0] = partial(d, u, 0, mine)
        to_mate(d, u, 0).wait_recv()
        acc[d, u, 0] += prt[d, u, 0]
        to_next(d, u, 0).start()
    for d, u in PAIRS:
        give(d, u, 1)

    def reduce_step(step, carry):
        for d, u in PAIRS:
            part = partial(d, u, step, mine)
            to_mate(d, u, step).wait_recv()
            to_next(d, u, step - 1).wait_recv()
            acc[d, u, step] += prt[d, u, step] + part
            to_next(d, u, step).start()
        for d, u in PAIRS:
            to_mate(d, u, step - 1).wait_send()
            give(d, u, step + 1)
        return carry

    lax.fori_loop(1, STEPS - 1, reduce_step, 0)
    last = STEPS - 1
    for d, u in PAIRS:
        part = partial(d, u, last, mine)
        to_mate(d, u, last).wait_recv()
        to_next(d, u, last - 1).wait_recv()
        acc[d, u, last] += prt[d, u, last] + part
        src = acc.at[d, u, last]
        gather_next(d, u, 0, src).start()
        gather_mate(d, u, 0, src).start()
        pltpu.make_async_copy(src, spread(d, u, 0), lo_sem.at[d, u]).start()

    for load in loads:
        load.wait()

    def gather_step(t, carry):
        for d, u in PAIRS:
            gather_next(d, u, t - 1, acc.at[d, u, last]).wait_recv()
            gather_next(d, u, t, spread(d, u, t)).start()
            gather_mate(d, u, t, spread(d, u, t)).start()
        block = pl.ds(pl.multiple_of(LANE * (t - 1), LANE), LANE)
        total = dot_nt(dq_ref[block, :], wq_ref[...]) + dot_nt(dk_ref[block, :], wk_ref[...]) + dot_nt(dv_ref[block, :], wv_ref[...])
        dxp_ref[block, :] = total.astype(BF)
        return carry

    lax.fori_loop(1, STEPS - 1, gather_step, 0)
    for d, u in PAIRS:
        gather_next(d, u, last - 1, acc.at[d, u, last]).wait_recv()
        gather_mate(d, u, last, spread(d, u, last)).start()

    unpermute_into(dxp_ref, dx_ref)

    def drain(t, carry):
        for d, u in PAIRS:
            to_next(d, u, t).wait_send()
            gather_next(d, u, t, acc.at[d, u, last]).wait_send()
            gather_mate(d, u, t, acc.at[d, u, last]).wait()
        return carry

    lax.fori_loop(0, last, drain, 0)
    for d, u in PAIRS:
        gather_mate(d, u, last, acc.at[d, u, last]).wait()
        to_mate(d, u, last - 1).wait_send()
        to_mate(d, u, last).wait_send()
        pltpu.make_async_copy(acc.at[d, u, last], spread(d, u, 0), lo_sem.at[d, u]).wait()


def ring_stage(xt, att, dq, dk, dv, dyp, wq, wk, wv):
    sem = lambda n: pltpu.SemaphoreType.DMA((2, 2, n))
    return pl.pallas_call(
        ring_kernel, name='ring_stage',
        in_specs=[pl.BlockSpec(memory_space=pltpu.VMEM)] * 6 + [pl.BlockSpec(memory_space=pl.ANY)] * 3,
        out_specs=[pl.BlockSpec(memory_space=pl.ANY)] * 4 + [pl.BlockSpec(memory_space=pltpu.VMEM)],
        out_shape=[jax.ShapeDtypeStruct((D, D), F32)] * 4 + [jax.ShapeDtypeStruct((T, D), BF)],
        scratch_shapes=[pltpu.VMEM((2, 2, STEPS, LANE, HALF), F32), pltpu.VMEM((2, 2, STEPS, LANE, HALF), F32), pltpu.VMEM((2, 2, 2, LANE, HALF), F32),
                        pltpu.VMEM((D, D), BF), pltpu.VMEM((D, D), BF), pltpu.VMEM((D, D), BF), pltpu.VMEM((T, D), BF),
                        sem(7), sem(7), sem(8), sem(8), sem(7), sem(7), sem(8), sem(8), pltpu.SemaphoreType.DMA((2, 2)), pltpu.SemaphoreType.DMA((3,))],
        compiler_params=pltpu.CompilerParams(has_side_effects=True, vmem_limit_bytes=63 * MIB),
       cost_estimate=cost(110),
    )(xt, att, dq, dk, dv, dyp, wq, wk, wv)


def solution(mesh):
    sp_size = mesh.shape['sp']

    def swap(a, bit):
        return lax.ppermute(a, 'sp', [(i, i ^ bit) for i in range(sp_size)])

    def device_work(x, w_q, w_k, w_v, w_o, dy):
        xt, dyp, q, k, v, do, sel = project(x, dy, w_q, w_k, w_v, w_o)
        sel8 = sel[:, ROWS:HALO]
        h2 = swap(sel8, 2)
        h1 = swap(sel, 1)
        h2, q = lax.optimization_barrier((h2, q))
        h3 = swap(h2, 1)
        grads, r1, r2 = (), [], []
        for half in range(2):
            *grads, one, two, three = attention(half, tuple(grads), q, k, v, do, h1, h2, h3)
            two = two + swap(three, 1)
            one, two, grads[0] = lax.optimization_barrier((one, two, grads[0]))
            r2.append(swap(two, 2))
            r1.append(swap(one, 1))
        at, dq, dk, dv = (g.reshape(T, D) for g in grads)
        y, att = out_stage(at, w_o)
        dkb, dvb = in_stage(dk, dv, *r1, *r2)
        dw_o, dw_q, dw_k, dw_v, dx = ring_stage(xt, att, dq, dkb, dvb, dyp, w_q, w_k, w_v)
        return y, dx, dw_q, dw_k, dw_v, dw_o

    row_spec = P(('dp', 'sp'), None)
    full_spec = P(None, None)
    grad_spec = P('dp', None)
    return jax.shard_map(device_work, mesh=mesh, in_specs=(row_spec, full_spec, full_spec, full_spec, full_spec, row_spec), out_specs=(row_spec, row_spec, grad_spec, grad_spec, grad_spec, grad_spec), check_vma=False)
```

time: 320 us -> 298 us (0.931)
  waiting for transfers between devices: 45 us -> 16.6 us
  other arithmetic: 0 us -> 3.61 us
    ppermute x6 -> x9, waiting for transfers between devices: 45 us -> 16.6 us  [swap(): return lax.ppermute(a, 'sp', [(i, i ^ bit) for i in range(sp_size)])]
    pallas_call x1, Pallas kernels: 12.6 us -> 6.17 us  [in_stage(): pl.pallas_call(in_kernel, grid=(4,), name='in_stage', in_specs=[tcol, tco...]
    pallas_call x2 -> x4, Pallas kernels: 54.9 us -> 60.4 us  [the longest x2 43.7 us: attention(): pl.pallas_call(body, grid=(4,), name='attention', in_specs=[row] * 4 + [b...]
    add x0 -> x2, other arithmetic: none -> 3.61 us  [device_work(): two = two + swap(three, 1)]
    unnamed x22 -> x19, local copies, waits for them, and re-layouts: 17.2 us -> 18.5 us
  transfers between devices with their start and end apart: 6 -> 9, of which waited for: 4 -> 6; matrix products, arithmetic and copies ran while one was open for 0% -> 1% of each run, Pallas kernels for 2% -> 5%
where the time goes in v4:
time: 298 us; the launch traced here: 297 us
  Pallas kernels  251 us (84%)
  local copies, waits for them, and re-layouts  19.5 us (7%)
  waiting for transfers between devices  16.6 us (6%)
  starting transfers between devices  6.01 us (2%)
  other arithmetic  3.61 us (1%)
    pallas_call x1, Pallas kernels, ring_stage(): pl.pallas_call(ring_kernel, name='ring_stage', in_specs=[pl.BlockSpec(mem...  177 us
    pallas_call x2, Pallas kernels, attention(): pl.pallas_call(body, grid=(4,), name='attention', in_specs=[row] * 4 + [b...  43.7 us
    unnamed x19, local copies, waits for them, and re-layouts  18.5 us
    ppermute x9, waiting for transfers between devices, swap(): return lax.ppermute(a, 'sp', [(i, i ^ bit) for i in range(sp_size)])  16.6 us
    pallas_call x1, Pallas kernels, project(): pl.pallas_call(queries_kernel, grid=(4,), name='project_queries', in_spec...  8.61 us
    pallas_call x1, Pallas kernels, project(): pl.pallas_call(keys_kernel, grid=(4,), name='project_keys', in_specs=[ful...  8.07 us
    pallas_call x1, Pallas kernels, out_stage(): pl.pallas_call(out_kernel, grid=(4,), name='out_stage', in_specs=[full, c...  7.47 us
    pallas_call x1, Pallas kernels, in_stage(): pl.pallas_call(in_kernel, grid=(4,), name='in_stage', in_specs=[tcol, tco...  6.17 us
  transfers between devices with their start and end apart: 9, of which 6 were waited for; matrix products, arithmetic and copies ran while one was open for 1% of the time, Pallas kernels for 5%

profile of v4, /device:TPU:0, one launch (start us, length us, event | category | flops | bytes accessed | tf_op | source)
XLA Modules:
  0.0 297.3 jit_solution(16927614631904047706)
XLA Ops:
  0.6 8.1 %project_keys.1 = (bf16[768,1024]{1,0:T(8,128)(2,1)}, bf16[768,1024]{1,0:T(8,128)(2,1)}, bf16[768,1024]{1,0:T(8,128)(2,1)}, bf16[2,288,1024]{2,1,0:T(8,128)(2,1)}) custom-call(bf16[768,1024]{1,0:T(8,128)(2,1)} %x_ref.1, bf16[1024,1024]{1,0:T(8,128)(2,1)} %wk_hbm.1, bf16[1024,1024]{1,0:T(8,128)(2,1)} %wv_hbm.1), custom_call_target="tpu_custom_call" | custom-call | flops 3300000000 | bytes 33000000 | tf_op jit(solution)/shard_map/project_keys/pallas_call | solution.py:110
  8.7 0.5 collective-permute-start.1
  9.2 1.0 slice.3
  10.2 2.6 collective-permute-start
  12.8 8.6 %project_queries.1 = (bf16[1024,768]{1,0:T(8,128)(2,1)}, bf16[768,1024]{1,0:T(8,128)(2,1)}, bf16[768,1024]{1,0:T(8,128)(2,1)}, bf16[768,1024]{1,0:T(8,128)(2,1)}) custom-call(bf16[768,1024]{1,0:T(8,128)(2,1)} %get-tuple-element.46.xp_ref, bf16[768,1024]{1,0:T(8,128)(2,1)} %dy_ref.1, bf16[1024,1024]{1,0:T(8,128)(2,1)} %wq_hbm.1, bf16[1024,1024]{1,0:T(8,128)(2,1)} %wo_ref.3), custom_call_target="tpu_custom_call" | custom-call | flops 3300000000 | bytes 33000000 | tf_op jit(solution)/shard_map/project_queries/pallas_call | solution.py:117
  21.4 1.2 collective-permute-done.refs_5_
  22.6 0.0 copy-start.5
  22.6 0.0 collective-permute-start.2
  22.6 1.7 collective-permute-done.2.refs_6_
  24.3 0.0 copy-start.6
  24.3 0.0 collective-permute-done.1.refs_4_
  24.3 0.0 copy-done.5
  24.3 0.7 copy-done.6
  25.1 21.7 %attention.2 = (bf16[8,2,48,1024]{3,2,1,0:T(8,128)(2,1)}, bf16[8,2,48,1024]{3,2,1,0:T(8,128)(2,1)}, f32[8,2,48,1024]{3,2,1,0:T(8,128)}, f32[8,2,48,1024]{3,2,1,0...) custom-call(bf16[8,2,48,1024]{3,2,1,0:T(8,128)(2,1)} %bitcast.14, ...), custom_call_target="tpu_custom_call" | custom-call | flops 15000000512 | bytes 150000000 | tf_op jit(solution)/shard_map/attention/pallas_call | solution.py:259
  46.8 0.2 collective-permute-start.3
  47.0 1.8 collective-permute-done.3
  48.8 1.8 add.6
  50.6 21.9 %attention.3 = (bf16[8,2,48,1024]{3,2,1,0:T(8,128)(2,1)}, bf16[8,2,48,1024]{3,2,1,0:T(8,128)(2,1)}, f32[8,2,48,1024]{3,2,1,0:T(8,128)}, f32[8,2,48,1024]{3,2,1,0...) custom-call(bf16[8,2,48,1024]{3,2,1,0:T(8,128)(2,1)} %bitcast.15, ...), custom_call_target="tpu_custom_call", output_to_operand_aliasing={{0}: (7, {}), {1}: (8, {}), {2}: (9, {}), {3}: (10, {})} | custom-call | flops 15000000512 | bytes 150000000 | tf_op jit(solution)/shard_map/attention/pallas_call | solution.py:259
  72.6 0.2 collective-permute-start.4
  72.8 0.4 collective-permute-start.5
  73.1 1.4 collective-permute-done.4
  74.6 1.8 add.7
  76.4 0.1 collective-permute-start.6
  76.5 1.8 collective-permute-start.7
  78.3 0.3 collective-permute-start.8
  78.5 7.5 %out_stage.1 = (bf16[768,1024]{1,0:T(8,128)(2,1)}, bf16[1024,768]{1,0:T(8,128)(2,1)}) custom-call(bf16[768,1024]{1,0:T(8,128)(2,1)} %bitcast.18, bf16[1024,1024]{1,0:T(8,128)(2,1)} %wo_ref.3), custom_call_target="tpu_custom_call" | custom-call | flops 1700000000 | bytes 17000000 | tf_op jit(solution)/shard_map/out_stage/pallas_call | solution.py:288
  86.0 2.7 collective-permute-done.7.r2a_ref
  88.7 0.0 copy-start.3
  88.7 7.8 %collective-permute-done.8.r2b_ref = f32[2,96,512]{2,1,0:T(8,128)S(1)} collective-permute-done((f32[2,96,512]{2,1,0:T(8,128)}, f32[2,96,512]{2,1,0:T(8,128)S(1)}, u32[]{:S(2)}, u32[]{:S(2)}) %collective-permute-start.8) | collective-permute-done | bytes 393248 | tf_op jit(solution)/shard_map/ppermute | solution.py:479
  96.5 0.0 copy-start.4
  96.5 0.0 collective-permute-done.5.r1a_ref
  96.5 0.0 collective-permute-done.6.r1b_ref
  96.5 0.0 copy-done.3
  96.5 0.7 copy-done.4
  97.3 6.2 %in_stage.1 = (bf16[768,1024]{1,0:T(8,128)(2,1)}, bf16[768,1024]{1,0:T(8,128)(2,1)}) custom-call(f32[768,1024]{1,0:T(8,128)} %bitcast.8, f32[768,1024]{1,0:T(8,128)} %bitcast.9, f32[2,288,512]{2,1,0:T(8,128)} %collective-permute-done.5.r1a_ref, f32[2,288,512]{2,1,0:T(8,128)} %collective-permute-done.6.r1b_ref, f32[2,96,512]{2,1,0:T(8,128)} %copy-done.3, ...), custom_call_target="tpu_custom_call" | custom-call | flops 100000000 | bytes 1000000 | tf_op jit(solution)/shard_map/in_stage/pallas_call | solution.py:321
  103.4 176.9 %ring_stage.1 = (f32[1024,1024]{1,0:T(8,128)}, f32[1024,1024]{1,0:T(8,128)}, f32[1024,1024]{1,0:T(8,128)}, f32[1024,1024]{1,0:T(8,128)}, bf16[768,1024]{1,0:T(8,128)(2,1)}) custom-call(bf16[1024,768]{1,0:T(8,128)(2,1)} %get-tuple-element.67.xt_ref, bf16[1024,768]{1,0:T(8,128)(2,1)} %get-tuple-element.68.att_ref, bf16[768,1024]{1,0:T(8,128)(2,1)} %bitcast.19, ...), custom_call_target="tpu_custom_call" | custom-call | flops 11000000512 | bytes 110000000 | tf_op jit(solution)/shard_map/ring_stage/pallas_call | solution.py:462
  280.3 2.7 copy.25
  283.0 0.0 copy-start.2
  283.0 4.9 %copy.26 = f32[1024,1024]{1,0:T(8,128)} copy(f32[1024,1024]{1,0:T(8,128)} %get-tuple-element.92) | data formatting | bytes 8388608
  287.9 0.0 copy-done.2
  287.9 0.0 copy-start.1
  287.9 2.1 copy.27
  290.0 1.6 copy-done.1
  291.6 0.0 copy-start
  291.6 2.1 copy.28
  293.7 1.6 copy-done
  295.3 2.0 copy.29
Async XLA Ops:
  8.7 15.6 %collective-permute-start.1 = (bf16[2,288,1024]{2,1,0:T(8,128)(2,1)}, bf16[2,288,1024]{2,1,0:T(8,128)(2,1)}, u32[]{:S(2)}, u32[]{:S(2)}) collective-permute-start(bf16[2,288,1024]{2,1,0:T(8,128)(2,1)} %get-tuple-element.45), channel_id=1, source_target_pairs={{0,1},{1,0},{2,3},{3,2},{4,5},{5,4},{6,7},{7,6},{8,9},{9,8},{10,11... | collective-permute-start | bytes 3538952 | tf_op jit(solution)/shard_map/ppermute | solution.py:479
  10.2 12.4 %collective-permute-start = (bf16[2,96,1024]{2,1,0:T(8,128)(2,1)S(1)}, bf16[2,96,1024]{2,1,0:T(8,128)(2,1)S(1)}, u32[]{:S(2)}, u32[]{:S(2)}) collective-permute-start(bf16[2,96,1024]{2,1,0:T(8,128)(2,1)S(1)} %slice.3), channel_id=1, source_target_pairs={{0,2},{1,3},{2,0},{3,1},{4,6},{5,7},{6,4},{7,5},{8,10},{9,11},{10,... | collective-permute-start | bytes 1179656 | tf_op jit(solution)/shard_map/ppermute | solution.py:479
  22.6 1.7 copy-start.5
  22.6 1.7 collective-permute-start.2
  24.3 0.7 copy-start.6
  46.8 2.0 collective-permute-start.3
  72.6 2.0 collective-permute-start.4
  72.8 23.8 %collective-permute-start.5 = (f32[2,288,512]{2,1,0:T(8,128)}, f32[2,288,512]{2,1,0:T(8,128)}, u32[]{:S(2)}, u32[]{:S(2)}) collective-permute-start(f32[2,288,512]{2,1,0:T(8,128)} %get-tuple-element.72), channel_id=1, source_target_pairs={{0,1},{1,0},{2,3},{3,2},{4,5},{5,4},{6,7},{7,6},{8,9},{9,8},{10,11... | collective-permute-start | bytes 3538952 | tf_op jit(solution)/shard_map/ppermute | solution.py:479
  76.4 20.2 %collective-permute-start.6 = (f32[2,288,512]{2,1,0:T(8,128)}, f32[2,288,512]{2,1,0:T(8,128)}, u32[]{:S(2)}, u32[]{:S(2)}) collective-permute-start(f32[2,288,512]{2,1,0:T(8,128)} %get-tuple-element.73), channel_id=1, source_target_pairs={{0,1},{1,0},{2,3},{3,2},{4,5},{5,4},{6,7},{7,6},{8,9},{9,8},{10,11... | collective-permute-start | bytes 3538952 | tf_op jit(solution)/shard_map/ppermute | solution.py:479
  76.5 12.2 %collective-permute-start.7 = (f32[2,96,512]{2,1,0:T(8,128)}, f32[2,96,512]{2,1,0:T(8,128)S(1)}, u32[]{:S(2)}, u32[]{:S(2)}) collective-permute-start(f32[2,96,512]{2,1,0:T(8,128)} %add.6), channel_id=1, source_target_pairs={{0,2},{1,3},{2,0},{3,1},{4,6},{5,7},{6,4},{7,5},{8,10},{9,11},{10,... | collective-permute-start | bytes 1179656 | tf_op jit(solution)/shard_map/ppermute | solution.py:479
  78.3 18.3 %collective-permute-start.8 = (f32[2,96,512]{2,1,0:T(8,128)}, f32[2,96,512]{2,1,0:T(8,128)S(1)}, u32[]{:S(2)}, u32[]{:S(2)}) collective-permute-start(f32[2,96,512]{2,1,0:T(8,128)} %add.7), channel_id=1, source_target_pairs={{0,2},{1,3},{2,0},{3,1},{4,6},{5,7},{6,4},{7,5},{8,10},{9,11},{10,... | collective-permute-start | bytes 1179656 | tf_op jit(solution)/shard_map/ppermute | solution.py:479
  88.7 7.8 %copy-start.3 = (f32[2,96,512]{2,1,0:T(8,128)}, f32[2,96,512]{2,1,0:T(8,128)S(1)}, u32[]{:S(2)}) copy-start(f32[2,96,512]{2,1,0:T(8,128)S(1)} %collective-permute-done.7.r2a_ref) | copy-start | bytes 1179652
  96.5 0.7 copy-start.4
  283.0 4.9 %copy-start.2 = (f32[1024,1024]{1,0:T(8,128)S(1)}, f32[1024,1024]{1,0:T(8,128)}, u32[]{:S(2)}) copy-start(f32[1024,1024]{1,0:T(8,128)} %get-tuple-element.93) | copy-start | bytes 12582916
  287.9 3.7 %copy-start.1 = (f32[1024,1024]{1,0:T(8,128)S(1)}, f32[1024,1024]{1,0:T(8,128)}, u32[]{:S(2)}) copy-start(f32[1024,1024]{1,0:T(8,128)} %get-tuple-element.94) | copy-start | bytes 12582916
  291.6 3.7 %copy-start = (f32[1024,1024]{1,0:T(8,128)S(1)}, f32[1024,1024]{1,0:T(8,128)}, u32[]{:S(2)}) copy-start(f32[1024,1024]{1,0:T(8,128)} %get-tuple-element.95) | copy-start | bytes 12582916

commit v5 on v4

--- a/solution.py
+++ b/solution.py
@@ -334,8 +334,8 @@
 
 
 def ring_kernel(xt_ref, att_ref, dq_ref, dk_ref, dv_ref, dy_ref, wq_hbm, wk_hbm, wv_hbm, *refs):
-    outs, dx_ref = refs[:4], refs[4]
-    acc, prt, stage, wq_ref, wk_ref, wv_ref, dxp_ref, rs_send, rs_recv, pt_send, pt_recv, ag_send, ag_recv, cc_send, cc_recv, lo_sem, ld_sem = refs[5:]
+    outs, dxp_ref = refs[:4], refs[4]
+    acc, prt, stage, wq_ref, wk_ref, wv_ref, rs_send, rs_recv, pt_send, pt_recv, ag_send, ag_recv, cc_send, cc_recv, lo_sem, ld_sem = refs[5:]
     loads = [pltpu.make_async_copy(a, b, ld_sem.at[n]) for n, (a, b) in enumerate(((wq_hbm, wq_ref), (wk_hbm, wk_ref), (wv_hbm, wv_ref)))]
     for load in loads:
         load.start()
@@ -440,8 +440,6 @@
         gather_next(d, u, last - 1, acc.at[d, u, last]).wait_recv()
         gather_mate(d, u, last, spread(d, u, last)).start()
 
-    unpermute_into(dxp_ref, dx_ref)
-
     def drain(t, carry):
         for d, u in PAIRS:
             to_next(d, u, t).wait_send()
@@ -465,11 +463,34 @@
         out_specs=[pl.BlockSpec(memory_space=pl.ANY)] * 4 + [pl.BlockSpec(memory_space=pltpu.VMEM)],
         out_shape=[jax.ShapeDtypeStruct((D, D), F32)] * 4 + [jax.ShapeDtypeStruct((T, D), BF)],
         scratch_shapes=[pltpu.VMEM((2, 2, STEPS, LANE, HALF), F32), pltpu.VMEM((2, 2, STEPS, LANE, HALF), F32), pltpu.VMEM((2, 2, 2, LANE, HALF), F32),
-                        pltpu.VMEM((D, D), BF), pltpu.VMEM((D, D), BF), pltpu.VMEM((D, D), BF), pltpu.VMEM((T, D), BF),
+                        pltpu.VMEM((D, D), BF), pltpu.VMEM((D, D), BF), pltpu.VMEM((D, D), BF),
                         sem(7), sem(7), sem(8), sem(8), sem(7), sem(7), sem(8), sem(8), pltpu.SemaphoreType.DMA((2, 2)), pltpu.SemaphoreType.DMA((3,))],
         compiler_params=pltpu.CompilerParams(has_side_effects=True, vmem_limit_bytes=63 * MIB),
        cost_estimate=cost(110),
     )(xt, att, dq, dk, dv, dyp, wq, wk, wv)
+
+
+def finish_kernel(a_ref, b_ref, c_ref, d_ref, dxp_ref, a_out, b_out, c_out, d_out, dx_ref):
+    j = pl.program_id(0)
+    for src, dst in ((a_ref, a_out), (b_ref, b_out), (c_ref, c_out), (d_ref, d_out)):
+        dst[...] = src[...]
+
+    @pl.when(j < T // LANE)
+    def _():
+        z = jnp.concatenate([dxp_ref[pl.ds(pl.multiple_of(c * CH + 16 * j, 16), 16), :] for c in range(8)], axis=0)
+        dx_ref[...] = dot(perm_matrix(True), z).astype(BF)
+
+
+def finish_stage(a, b, c, d, dxp):
+    block = pl.BlockSpec((LANE, D), lambda j: (j, 0))
+    return pl.pallas_call(
+        finish_kernel, grid=(8,), name='finish_stage',
+        in_specs=[block] * 4 + [pl.BlockSpec((T, D), lambda j: (0, 0))],
+        out_specs=[block] * 4 + [pl.BlockSpec((LANE, D), lambda j: (jnp.minimum(j, T // LANE - 1), 0))],
+        out_shape=[jax.ShapeDtypeStruct((D, D), F32)] * 4 + [jax.ShapeDtypeStruct((T, D), BF)],
+        compiler_params=pltpu.CompilerParams(vmem_limit_bytes=63 * MIB),
+       cost_estimate=cost(2),
+    )(a, b, c, d, dxp)
 
 
 def solution(mesh):
@@ -495,7 +516,7 @@
         at, dq, dk, dv = (g.reshape(T, D) for g in grads)
         y, att = out_stage(at, w_o)
         dkb, dvb = in_stage(dk, dv, *r1, *r2)
-        dw_o, dw_q, dw_k, dw_v, dx = ring_stage(xt, att, dq, dkb, dvb, dyp, w_q, w_k, w_v)
+        dw_o, dw_q, dw_k, dw_v, dx = finish_stage(*ring_stage(xt, att, dq, dkb, dvb, dyp, w_q, w_k, w_v))
         return y, dx, dw_q, dw_k, dw_v, dw_o
 
     row_spec = P(('dp', 'sp'), None)

time: 298 us -> 296 us (level)
  local copies, waits for them, and re-layouts: 19.5 us -> 2.51 us
  Pallas kernels: 251 us -> 266 us
    unnamed x19 -> x8, local copies, waits for them, and re-layouts: 18.5 us -> 1.49 us
    pallas_call x0 -> x1, Pallas kernels: none -> 15.2 us  [finish_stage(): pl.pallas_call(finish_kernel, grid=(8,), name='finish_stage', in_specs=[b...]
where the time goes in v5:
time: 296 us
  Pallas kernels  266 us (90%)
  waiting for transfers between devices  16.6 us (6%)
  starting transfers between devices  6.04 us (2%)
  other arithmetic  3.63 us (1%)
    pallas_call x1, Pallas kernels, ring_stage(): pl.pallas_call(ring_kernel, name='ring_stage', in_specs=[pl.BlockSpec(mem...  177 us
    pallas_call x2, Pallas kernels, attention(): pl.pallas_call(body, grid=(4,), name='attention', in_specs=[row] * 4 + [b...  43.7 us
    ppermute x9, waiting for transfers between devices, swap(): return lax.ppermute(a, 'sp', [(i, i ^ bit) for i in range(sp_size)])  16.6 us
    pallas_call x1, Pallas kernels, finish_stage(): pl.pallas_call(finish_kernel, grid=(8,), name='finish_stage', in_specs=[b...  15.2 us
    pallas_call x1, Pallas kernels, project(): pl.pallas_call(queries_kernel, grid=(4,), name='project_queries', in_spec...  8.61 us
    pallas_call x1, Pallas kernels, project(): pl.pallas_call(keys_kernel, grid=(4,), name='project_keys', in_specs=[ful...  8.07 us
    pallas_call x1, Pallas kernels, out_stage(): pl.pallas_call(out_kernel, grid=(4,), name='out_stage', in_specs=[full, c...  7.47 us
    pallas_call x1, Pallas kernels, in_stage(): pl.pallas_call(in_kernel, grid=(4,), name='in_stage', in_specs=[tcol, tco...  6.19 us
  transfers between devices with their start and end apart: 9, of which 6 were waited for; matrix products, arithmetic and copies ran while one was open for 1% of the time, Pallas kernels for 5%

profile of v5, /device:TPU:0, one launch (start us, length us, event | category | flops | bytes accessed | tf_op | source)
XLA Modules:
  0.0 295.7 jit_solution(12822299637432176749)
XLA Ops:
  0.6 8.1 %project_keys.1 = (bf16[768,1024]{1,0:T(8,128)(2,1)}, bf16[768,1024]{1,0:T(8,128)(2,1)}, bf16[768,1024]{1,0:T(8,128)(2,1)}, bf16[2,288,1024]{2,1,0:T(8,128)(2,1)}) custom-call(bf16[768,1024]{1,0:T(8,128)(2,1)} %x_ref.1, bf16[1024,1024]{1,0:T(8,128)(2,1)} %wk_hbm.1, bf16[1024,1024]{1,0:T(8,128)(2,1)} %wv_hbm.1), custom_call_target="tpu_custom_call" | custom-call | flops 3300000000 | bytes 33000000 | tf_op jit(solution)/shard_map/project_keys/pallas_call | solution.py:110
  8.7 0.5 collective-permute-start.1
  9.2 1.0 slice.3
  10.2 2.6 collective-permute-start
  12.8 8.6 %project_queries.1 = (bf16[1024,768]{1,0:T(8,128)(2,1)}, bf16[768,1024]{1,0:T(8,128)(2,1)}, bf16[768,1024]{1,0:T(8,128)(2,1)}, bf16[768,1024]{1,0:T(8,128)(2,1)}) custom-call(bf16[768,1024]{1,0:T(8,128)(2,1)} %get-tuple-element.51.xp_ref, bf16[768,1024]{1,0:T(8,128)(2,1)} %dy_ref.1, bf16[1024,1024]{1,0:T(8,128)(2,1)} %wq_hbm.1, bf16[1024,1024]{1,0:T(8,128)(2,1)} %wo_ref.3), custom_call_target="tpu_custom_call" | custom-call | flops 3300000000 | bytes 33000000 | tf_op jit(solution)/shard_map/project_queries/pallas_call | solution.py:117
  21.4 1.2 collective-permute-done.refs_5_
  22.6 0.0 copy-start.2
  22.6 0.0 collective-permute-start.2
  22.6 1.7 collective-permute-done.2.refs_6_
  24.3 0.0 copy-start.3
  24.3 0.0 collective-permute-done.1.refs_4_
  24.3 0.0 copy-done.2
  24.3 0.7 copy-done.3
  25.1 21.7 %attention.2 = (bf16[8,2,48,1024]{3,2,1,0:T(8,128)(2,1)}, bf16[8,2,48,1024]{3,2,1,0:T(8,128)(2,1)}, f32[8,2,48,1024]{3,2,1,0:T(8,128)}, f32[8,2,48,1024]{3,2,1,0...) custom-call(bf16[8,2,48,1024]{3,2,1,0:T(8,128)(2,1)} %bitcast.14, ...), custom_call_target="tpu_custom_call" | custom-call | flops 15000000512 | bytes 150000000 | tf_op jit(solution)/shard_map/attention/pallas_call | solution.py:259
  46.8 0.2 collective-permute-start.3
  47.0 1.8 collective-permute-done.3
  48.8 1.8 add.6
  50.6 21.9 %attention.3 = (bf16[8,2,48,1024]{3,2,1,0:T(8,128)(2,1)}, bf16[8,2,48,1024]{3,2,1,0:T(8,128)(2,1)}, f32[8,2,48,1024]{3,2,1,0:T(8,128)}, f32[8,2,48,1024]{3,2,1,0...) custom-call(bf16[8,2,48,1024]{3,2,1,0:T(8,128)(2,1)} %bitcast.15, ...), custom_call_target="tpu_custom_call", output_to_operand_aliasing={{0}: (7, {}), {1}: (8, {}), {2}: (9, {}), {3}: (10, {})} | custom-call | flops 15000000512 | bytes 150000000 | tf_op jit(solution)/shard_map/attention/pallas_call | solution.py:259
  72.6 0.2 collective-permute-start.4
  72.8 0.4 collective-permute-start.5
  73.1 1.4 collective-permute-done.4
  74.6 1.8 add.7
  76.4 0.2 collective-permute-start.6
  76.5 1.7 collective-permute-start.7
  78.3 0.3 collective-permute-start.8
  78.5 7.5 %out_stage.1 = (bf16[768,1024]{1,0:T(8,128)(2,1)}, bf16[1024,768]{1,0:T(8,128)(2,1)}) custom-call(bf16[768,1024]{1,0:T(8,128)(2,1)} %bitcast.18, bf16[1024,1024]{1,0:T(8,128)(2,1)} %wo_ref.3), custom_call_target="tpu_custom_call" | custom-call | flops 1700000000 | bytes 17000000 | tf_op jit(solution)/shard_map/out_stage/pallas_call | solution.py:288
  86.0 2.7 collective-permute-done.7.r2a_ref
  88.7 0.0 copy-start
  88.7 7.8 %collective-permute-done.8.r2b_ref = f32[2,96,512]{2,1,0:T(8,128)S(1)} collective-permute-done((f32[2,96,512]{2,1,0:T(8,128)}, f32[2,96,512]{2,1,0:T(8,128)S(1)}, u32[]{:S(2)}, u32[]{:S(2)}) %collective-permute-start.8) | collective-permute-done | bytes 393248 | tf_op jit(solution)/shard_map/ppermute | solution.py:500
  96.5 0.0 copy-start.1
  96.6 0.0 collective-permute-done.5.r1a_ref
  96.6 0.0 collective-permute-done.6.r1b_ref
  96.6 0.0 copy-done
  96.6 0.7 copy-done.1
  97.3 6.2 %in_stage.1 = (bf16[768,1024]{1,0:T(8,128)(2,1)}, bf16[768,1024]{1,0:T(8,128)(2,1)}) custom-call(f32[768,1024]{1,0:T(8,128)} %bitcast.8, f32[768,1024]{1,0:T(8,128)} %bitcast.9, f32[2,288,512]{2,1,0:T(8,128)} %collective-permute-done.5.r1a_ref, f32[2,288,512]{2,1,0:T(8,128)} %collective-permute-done.6.r1b_ref, f32[2,96,512]{2,1,0:T(8,128)} %copy-done, ...), custom_call_target="tpu_custom_call" | custom-call | flops 100000000 | bytes 1000000 | tf_op jit(solution)/shard_map/in_stage/pallas_call | solution.py:321
  103.5 176.9 %ring_stage.1 = (f32[1024,1024]{1,0:T(8,128)}, f32[1024,1024]{1,0:T(8,128)}, f32[1024,1024]{1,0:T(8,128)}, f32[1024,1024]{1,0:T(8,128)}, bf16[768,1024]{1,0:T(8,128)(2,1)}) custom-call(bf16[1024,768]{1,0:T(8,128)(2,1)} %get-tuple-element.72.xt_ref, bf16[1024,768]{1,0:T(8,128)(2,1)} %get-tuple-element.73.att_ref, bf16[768,1024]{1,0:T(8,128)(2,1)} %bitcast.19, ...), custom_call_target="tpu_custom_call" | custom-call | flops 11000000512 | bytes 110000000 | tf_op jit(solution)/shard_map/ring_stage/pallas_call | solution.py:460
  280.4 15.2 %finish_stage.1 = (f32[1024,1024]{1,0:T(8,128)}, f32[1024,1024]{1,0:T(8,128)}, f32[1024,1024]{1,0:T(8,128)}, f32[1024,1024]{1,0:T(8,128)}, bf16[768,1024]{1,0:T(8,128)(2,1)}) custom-call(f32[1024,1024]{1,0:T(8,128)} %get-tuple-element.84.a_ref, f32[1024,1024]{1,0:T(8,128)} %get-tuple-element.85.b_ref, f32[1024,1024]{1,0:T(8,128)} %get-tuple-element.86.c_ref, ...), custom_call_target="tpu_custom_call" | custom-call | flops 200000000 | bytes 2000000 | tf_op jit(solution)/shard_map/finish_stage/pallas_call | solution.py:486
Async XLA Ops:
  8.7 15.6 %collective-permute-start.1 = (bf16[2,288,1024]{2,1,0:T(8,128)(2,1)}, bf16[2,288,1024]{2,1,0:T(8,128)(2,1)}, u32[]{:S(2)}, u32[]{:S(2)}) collective-permute-start(bf16[2,288,1024]{2,1,0:T(8,128)(2,1)} %get-tuple-element.50), channel_id=1, source_target_pairs={{0,1},{1,0},{2,3},{3,2},{4,5},{5,4},{6,7},{7,6},{8,9},{9,8},{10,11... | collective-permute-start | bytes 3538952 | tf_op jit(solution)/shard_map/ppermute | solution.py:500
  10.2 12.4 %collective-permute-start = (bf16[2,96,1024]{2,1,0:T(8,128)(2,1)S(1)}, bf16[2,96,1024]{2,1,0:T(8,128)(2,1)S(1)}, u32[]{:S(2)}, u32[]{:S(2)}) collective-permute-start(bf16[2,96,1024]{2,1,0:T(8,128)(2,1)S(1)} %slice.3), channel_id=1, source_target_pairs={{0,2},{1,3},{2,0},{3,1},{4,6},{5,7},{6,4},{7,5},{8,10},{9,11},{10,... | collective-permute-start | bytes 1179656 | tf_op jit(solution)/shard_map/ppermute | solution.py:500
  22.6 1.7 copy-start.2
  22.6 1.7 collective-permute-start.2
  24.3 0.8 copy-start.3
  46.8 2.0 collective-permute-start.3
  72.6 2.0 collective-permute-start.4
  72.8 23.8 %collective-permute-start.5 = (f32[2,288,512]{2,1,0:T(8,128)}, f32[2,288,512]{2,1,0:T(8,128)}, u32[]{:S(2)}, u32[]{:S(2)}) collective-permute-start(f32[2,288,512]{2,1,0:T(8,128)} %get-tuple-element.77), channel_id=1, source_target_pairs={{0,1},{1,0},{2,3},{3,2},{4,5},{5,4},{6,7},{7,6},{8,9},{9,8},{10,11... | collective-permute-start | bytes 3538952 | tf_op jit(solution)/shard_map/ppermute | solution.py:500
  76.4 20.2 %collective-permute-start.6 = (f32[2,288,512]{2,1,0:T(8,128)}, f32[2,288,512]{2,1,0:T(8,128)}, u32[]{:S(2)}, u32[]{:S(2)}) collective-permute-start(f32[2,288,512]{2,1,0:T(8,128)} %get-tuple-element.78), channel_id=1, source_target_pairs={{0,1},{1,0},{2,3},{3,2},{4,5},{5,4},{6,7},{7,6},{8,9},{9,8},{10,11... | collective-permute-start | bytes 3538952 | tf_op jit(solution)/shard_map/ppermute | solution.py:500
  76.5 12.2 %collective-permute-start.7 = (f32[2,96,512]{2,1,0:T(8,128)}, f32[2,96,512]{2,1,0:T(8,128)S(1)}, u32[]{:S(2)}, u32[]{:S(2)}) collective-permute-start(f32[2,96,512]{2,1,0:T(8,128)} %add.6), channel_id=1, source_target_pairs={{0,2},{1,3},{2,0},{3,1},{4,6},{5,7},{6,4},{7,5},{8,10},{9,11},{10,... | collective-permute-start | bytes 1179656 | tf_op jit(solution)/shard_map/ppermute | solution.py:500
  78.3 18.3 %collective-permute-start.8 = (f32[2,96,512]{2,1,0:T(8,128)}, f32[2,96,512]{2,1,0:T(8,128)S(1)}, u32[]{:S(2)}, u32[]{:S(2)}) collective-permute-start(f32[2,96,512]{2,1,0:T(8,128)} %add.7), channel_id=1, source_target_pairs={{0,2},{1,3},{2,0},{3,1},{4,6},{5,7},{6,4},{7,5},{8,10},{9,11},{10,... | collective-permute-start | bytes 1179656 | tf_op jit(solution)/shard_map/ppermute | solution.py:500
  88.7 7.8 %copy-start = (f32[2,96,512]{2,1,0:T(8,128)}, f32[2,96,512]{2,1,0:T(8,128)S(1)}, u32[]{:S(2)}) copy-start(f32[2,96,512]{2,1,0:T(8,128)S(1)} %collective-permute-done.7.r2a_ref) | copy-start | bytes 1179652
  96.5 0.8 copy-start.1
